TPU v7x, 128 devices: a whole 4x4x4 slice. The times are simulated.
128 devices in a mesh: row: 8 (over x, core), col: 16 (over y, z).
Axes of the slice: x: 4, y: 4, z: 4, core: 2. Of those that a mesh axis runs over, the one named last changes fastest.
Arguments:
- solution: float32 [49152, 128], P(('row', 'col')), may hold values from -6 to 6
- right_side: float32 [49152, 128], P(('row', 'col')), may hold values from -6 to 6
- block_values: bfloat16 [384, 64, 128, 128], P('row', 'col'), may hold values from -0.0625 to 0.0625
- block_columns: int32 [384, 64], P('row', 'col'), may hold values from 0 to 383, as said below
- row_order: int32 [49152], P(('row', 'col')), may hold values from 0 to 49151, as said below
- tri_inverses: bfloat16 [16384, 28672], P(('row', 'col')), may hold values from -1 to 2
- lower_updates: bfloat16 [12288, 16384], P(None, ('row', 'col')), may hold values from -0.0625 to 0.0625
- upper_updates: bfloat16 [16384, 12288], P(('row', 'col')), may hold values from -0.0625 to 0.0625
- update_rows: int32 [2, 16384], replicated, may hold values from 0 to 16383, as said below
Outputs:
- refined: float32 [49152, 128], P(('row', 'col'))
- residual: float32 [49152, 128], P(('row', 'col'))
Inputs may be any that keep to these rules, and one draw needn't show every extreme that they name: `block_columns`: for block row i and slot s, the named block b satisfies (b // 3) % (16) == s // 4. `row_order`: each aligned block of 384 entries is a permutation of that block's own positions. `update_rows`: in row k, each aligned block of 2^k * 4096 entries holds distinct values below 2^(k+1) * 4096.
All inputs are finite; a program needn't handle non-finite values.
Results may differ from a plain program's by a relative error of at most 0.02.
Values may be sent and summed in bfloat16 or wider, within the bound.
A program may use at most 128 MiB of HBM per device.

v0:
```python
import jax
import jax.numpy as jnp
from jax import lax
from jax.sharding import PartitionSpec as P


def split_up(x, dim, length):
    lengths = x.shape
    blocks = x.reshape(*lengths[:dim], length, lengths[dim] // length, *lengths[dim + 1 :])
    return jnp.moveaxis(blocks, dim, 0)


def summed_on_arrival(x, axis, dim):
    blocks = split_up(x, dim, lax.axis_size(axis))
    arrived = lax.all_to_all(blocks, axis, split_axis=0, concat_axis=0, tiled=True)
    return arrived.sum(axis=0)


def laid_out(blocks, dim):
    blocks = jnp.moveaxis(blocks, 0, dim)
    lengths = blocks.shape
    return blocks.reshape(*lengths[:dim], lengths[dim] * lengths[dim + 1], *lengths[dim + 2 :])


def sent_to_all(x, axis):
    copies = jnp.broadcast_to(x, (lax.axis_size(axis), *x.shape))
    return lax.all_to_all(copies, axis, split_axis=0, concat_axis=0, tiled=True)


def collect(x, axis, dim):
    return laid_out(sent_to_all(x, axis), dim)


def from_partner(block, axis, distance):
    count = lax.axis_size(axis)
    route = []
    for low in range(count):
        high = low | 1 << distance
        if high != low and high < count:
            route += [(low, high), (high, low)]
    return lax.ppermute(block, axis, route)


def column_sum(values):
    return summed_on_arrival(values, "col", 0)


def column_gather(values):
    return collect(values, "col", 0)


def partner_values(values, bit_index):
    return from_partner(values, "row", bit_index)


def partner_totals(values, bit_index):
    return from_partner(values.astype(jnp.bfloat16), "row", bit_index).astype(values.dtype)


def join_rows(values, bit_count):
    position = lax.axis_index("row")
    for bit_index in range(bit_count):
        partner = partner_values(values, bit_index)
        raised = position >> bit_index & 1 == 1
        values = jnp.where(
            raised, jnp.concatenate([partner, values], 0), jnp.concatenate([values, partner], 0)
        )
    return values


def halve_rows(values, bit_count):
    position = lax.axis_index("row")
    for bit_index in reversed(range(bit_count)):
        middle = values.shape[0] // 2
        raised = position >> bit_index & 1 == 1
        retained = jnp.where(raised, values[middle:], values[:middle])
        outgoing = jnp.where(raised, values[:middle], values[middle:])
        values = retained + partner_totals(outgoing, bit_index)
    return values


def front_gather(values, bit_count):
    joined = join_rows(values, bit_count)
    spread = column_gather(joined)
    col_count = lax.axis_size("col")
    col_grid = spread.reshape(col_count, 2**bit_count, values.shape[0], values.shape[1])
    return jnp.swapaxes(col_grid, 0, 1).reshape(-1, values.shape[1])


def front_reduce(targets, partials, bit_count, seg_rows):
    col_count = lax.axis_size("col")
    group_rows = 2**bit_count
    total_rows = group_rows * col_count * seg_rows
    zeros_sum = jnp.zeros((total_rows, partials.shape[1]), jnp.float32)
    dense_grid = zeros_sum.at[targets].add(partials).reshape(group_rows, col_count * seg_rows, -1)
    return column_sum(halve_rows(dense_grid, bit_count)[0])


def triangle_rows(tri_panel, full_vector, first_row, strict_lower):
    row_ids = first_row + lax.broadcasted_iota(jnp.int32, tri_panel.shape, 0)
    col_ids = lax.broadcasted_iota(jnp.int32, tri_panel.shape, 1)
    keep_mask = col_ids < row_ids if strict_lower else col_ids >= row_ids
    masked = jnp.where(keep_mask, tri_panel, jnp.zeros_like(tri_panel))
    return jnp.dot(masked, full_vector, preferred_element_type=jnp.float32)


def on_device(
    solution,
    right_side,
    block_values,
    block_columns,
    row_order,
    tri_inverses,
    lower_updates,
    upper_updates,
    update_rows,
):
    row_count = lax.axis_size("row")
    col_count = lax.axis_size("col")
    levels_count = row_count.bit_length() - 1
    per_device = solution.shape[0]
    seg_rows = per_device // levels_count
    block_size = block_values.shape[2]
    per_block = per_device // block_size
    row_index = lax.axis_index("row")
    col_index = lax.axis_index("col")
    gathered = collect(solution.astype(jnp.bfloat16), "row", 0).astype(solution.dtype)
    local_block = block_columns // (per_block * col_count) * per_block + block_columns % per_block
    solution_blocks = gathered.reshape(row_count * per_block, block_size, -1)
    picked = solution_blocks[local_block]
    applied = jnp.einsum(
        "iskl,isln->ikn", block_values.astype(jnp.float32), picked, precision=lax.Precision.HIGHEST
    )
    product = column_sum(applied.reshape(-1, applied.shape[-1]))
    residual = right_side - product
    device_index = row_index * col_count + col_index
    local_order = row_order - device_index * per_device
    permuted = residual[local_order]
    stacked = permuted.reshape(levels_count, seg_rows, -1)
    sep_bottom = 2 * col_count * seg_rows
    lowered = []
    targets_all = []
    first_rows = []
    incoming = None
    for depth_k in range(levels_count):
        groups = 2 ** (depth_k + 1)
        span_rows = sep_bottom * 2**depth_k
        offset_col = sep_bottom * (2**depth_k - 1)
        first_row = (row_index % groups * col_count + col_index) * seg_rows
        first_rows.append(first_row)
        current = stacked[depth_k]
        if depth_k > 0:
            current = current - incoming
        rounded = current.astype(jnp.bfloat16)
        front_full = front_gather(rounded, depth_k + 1)
        tri_panel = tri_inverses[:, offset_col : offset_col + span_rows]
        solved_rows = triangle_rows(tri_panel, front_full, first_row, True) + rounded.astype(
            jnp.float32
        )
        lower_rows = solved_rows.astype(jnp.bfloat16)
        lowered.append(lower_rows)
        if depth_k + 1 < levels_count:
            front_idx = row_index // groups
            chosen = lax.dynamic_slice_in_dim(
                update_rows[depth_k], front_idx * span_rows, span_rows
            )
            targets_all.append(chosen)
            partials = jnp.dot(
                lower_updates[offset_col : offset_col + span_rows],
                lower_rows,
                preferred_element_type=jnp.float32,
            )
            incoming = front_reduce(chosen, partials, depth_k + 2, seg_rows)
    corrections = [None] * levels_count
    parent_rows = None
    for depth_k in reversed(range(levels_count)):
        span_rows = sep_bottom * 2**depth_k
        offset_col = sep_bottom * (2**depth_k - 1)
        reduced = lowered[depth_k].astype(jnp.float32)
        if depth_k + 1 < levels_count:
            parent_full = front_gather(parent_rows, depth_k + 2)
            picked_rows = parent_full[targets_all[depth_k]]
            reduced = reduced - jnp.dot(
                upper_updates[:, offset_col : offset_col + span_rows],
                picked_rows,
                preferred_element_type=jnp.float32,
            )
        rounded = reduced.astype(jnp.bfloat16)
        full_vector = front_gather(rounded, depth_k + 1)
        tri_panel = tri_inverses[:, offset_col : offset_col + span_rows]
        upper_rows = triangle_rows(tri_panel, full_vector, first_rows[depth_k], False)
        corrections[depth_k] = upper_rows
        parent_rows = upper_rows.astype(jnp.bfloat16)
    correction = jnp.concatenate(corrections, 0)
    return (solution + correction, residual)


def solution(mesh):
    in_specs = (
        P(("row", "col"), None),
        P(("row", "col"), None),
        P("row", "col", None, None),
        P("row", "col"),
        P(("row", "col")),
        P(("row", "col"), None),
        P(None, ("row", "col")),
        P(("row", "col"), None),
        P(),
    )
    out_specs = (P(("row", "col"), None), P(("row", "col"), None))
    return jax.shard_map(
        on_device, mesh=mesh, in_specs=in_specs, out_specs=out_specs, check_vma=False
    )
```

profile of v0, /device:TPU:1, one launch (start us, length us, event | category | flops | bytes accessed | tf_op | source)
XLA Modules:
  0.0 777.5 jit_solution(6996237839127744655)
XLA Ops:
  2.6 5.8 all-to-all-start
  9.3 11.3 %all-to-all-done = bf16[8,384,128]{2,1,0:T(8,128)(2,1)S(1)} async-done(((bf16[8,384,128]{2,1,0:T(8,128)(2,1)}), bf16[8,384,128]{2,1,0:T(8,128)(2,1)S(1)}, u32[]{:S(2)}, u32[]{:S(2)}) %all-to-all-start) | async-done | bytes 786464 | tf_op jit(solution)/shard_map/all_to_all | solution.py:27
  20.5 8.0 %gather_fusion = bf16[192,128,128]{2,1,0:T(8,128)(2,1)} fusion(bf16[24,128,128]{2,1,0:T(8,128)(2,1)S(1)} %bitcast.81, s32[1024]{0:T(1024)S(1)} %pad_clamp_fusion.1), kind=kCustom, calls=%fused_computation | custom fusion | bytes 12583680 | tf_op jit(solution)/shard_map/gather | solution.py:130
  28.5 8.1 %fusion.81 = f32[48,128,128,1]{1,2,3,0:T(8,128)} fusion(bf16[48,4,128,128]{3,2,1,0:T(8,128)(2,1)} %param.11, bf16[48,4,128,128]{3,2,1,0:T(8,128)(2,1)} %bitcast.83), kind=kOutput, calls=%fused_computation.126 | convolution fusion | flops 805306368 | bytes 15728640 | tf_op jit(solution)/shard_map/iskl,isln->ikn/dot_general | solution.py:131
  36.7 7.9 %all-to-all-start.1 = ((f32[16,384,128]{2,1,0:T(8,128)}), f32[16,384,128]{2,1,0:T(8,128)S(1)}, u32[]{:S(2)}, u32[]{:S(2)}) async-start(f32[16,384,128]{2,1,0:T(8,128)} %bitcast.5), calls=%async_computation.1 | async-start | bytes 6291456 | tf_op jit(solution)/shard_map/all_to_all | solution.py:15
  44.6 40.5 %all-to-all-done.1 = f32[16,384,128]{2,1,0:T(8,128)S(1)} async-done(((f32[16,384,128]{2,1,0:T(8,128)}), f32[16,384,128]{2,1,0:T(8,128)S(1)}, u32[]{:S(2)}, u32[]{:S(2)}) %all-to-all-start.1) | async-done | bytes 3145760 | tf_op jit(solution)/shard_map/all_to_all | solution.py:15
  86.5 3.6 collective-permute-start
  92.2 5.2 all-to-all-start.2
  97.6 15.5 %all-to-all-done.2 = bf16[16,256,128]{2,1,0:T(8,128)(2,1)S(1)} async-done(((bf16[16,256,128]{2,1,0:T(8,128)(2,1)}), bf16[16,256,128]{2,1,0:T(8,128)(2,1)S(1)}, u32[]{:S(2)}, u32[]{:S(2)}) %all-to-all-start.2) | async-done | bytes 1048608 | tf_op jit(solution)/shard_map/all_to_all | solution.py:27
  118.4 24.8 %scatter_custom_fusion = f32[8192,128]{1,0:T(8,128)} fusion(s32[4096]{0:T(1024)S(1)} %bitcast.104, f32[4096,128]{1,0:T(8,128)} %copy.20, f32[]{:T(128)} %constant.105.clone.1), kind=kCustom, calls=%fused_computation.38 | custom fusion | flops 524288 | bytes 4194816 | tf_op jit(solution)/shard_map/scatter-add | solution.py:95
  148.5 18.9 %collective-permute-done.1 = bf16[2,2048,128]{2,1,0:T(8,128)(2,1)S(1)} collective-permute-done((bf16[2,2048,128]{2,1,0:T(8,128)(2,1)S(1)}, bf16[2,2048,128]{2,1,0:T(8,128)(2,1)S(1)}, u32[]{:S(2)}, u32[]{:S(2)}) %collective-permute-start.1) | collective-permute-done | bytes 1048608 | tf_op jit(solution)/shard_map/ppermute | solution.py:41
  167.7 4.0 collective-permute-start.2
  173.4 20.3 %all_to_all.60 = f32[16,128,128]{2,1,0:T(8,128)S(1)} all-to-all(f32[16,128,128]{2,1,0:T(8,128)S(1)} %bitcast.94), channel_id=1, replica_groups=mesh['row'=8,'col'=16] {'col'}, dimensions={0} | all-to-all | bytes 2097152 | tf_op jit(solution)/shard_map/all_to_all | solution.py:15
  202.1 3.7 all-to-all-start.4
  205.9 25.8 %all-to-all-done.4 = bf16[16,512,128]{2,1,0:T(8,128)(2,1)S(1)} async-done(((bf16[16,512,128]{2,1,0:T(8,128)(2,1)}), bf16[16,512,128]{2,1,0:T(8,128)(2,1)S(1)}, u32[]{:S(2)}, u32[]{:S(2)}) %all-to-all-start.4) | async-done | bytes 2097184 | tf_op jit(solution)/shard_map/all_to_all | solution.py:27
  237.1 5.6 copy.22
  242.7 48.1 %scatter_custom_fusion.1 = f32[16384,128]{1,0:T(8,128)} fusion(s32[8192]{0:T(1024)S(1)} %bitcast.102, f32[8192,128]{1,0:T(8,128)} %copy.22, f32[]{:T(128)} %constant.105.clone.1), kind=kCustom, calls=%fused_computation.16 | custom fusion | flops 1048576 | bytes 8389120 | tf_op jit(solution)/shard_map/scatter-add | solution.py:95
  290.8 3.8 select_convert_fusion
  296.9 3.9 slice_select_fusion
  300.8 37.6 %collective-permute-done.5 = bf16[4,2048,128]{2,1,0:T(8,128)(2,1)S(1)} collective-permute-done((bf16[4,2048,128]{2,1,0:T(8,128)(2,1)S(1)}, bf16[4,2048,128]{2,1,0:T(8,128)(2,1)S(1)}, u32[]{:S(2)}, u32[]{:S(2)}) %collective-permute-start.5) | collective-permute-done | bytes 2097184 | tf_op jit(solution)/shard_map/ppermute | solution.py:41
  339.3 21.1 %collective-permute-done.6 = bf16[2,2048,128]{2,1,0:T(8,128)(2,1)S(1)} collective-permute-done((bf16[2,2048,128]{2,1,0:T(8,128)(2,1)S(1)}, bf16[2,2048,128]{2,1,0:T(8,128)(2,1)S(1)}, u32[]{:S(2)}, u32[]{:S(2)}) %collective-permute-start.6) | collective-permute-done | bytes 1048608 | tf_op jit(solution)/shard_map/ppermute | solution.py:41
  360.9 5.0 collective-permute-start.7
  367.7 23.6 %all_to_all.61 = f32[16,128,128]{2,1,0:T(8,128)S(1)} all-to-all(f32[16,128,128]{2,1,0:T(8,128)S(1)} %bitcast.95), channel_id=1, replica_groups=mesh['row'=8,'col'=16] {'col'}, dimensions={0} | all-to-all | bytes 2097152 | tf_op jit(solution)/shard_map/all_to_all | solution.py:15
  400.0 3.1 collective-permute-done.10
  403.1 2.8 broadcast_in_dim.50
  405.9 14.3 %all-to-all-start.6 = ((bf16[16,1024,128]{2,1,0:T(8,128)(2,1)}), bf16[16,1024,128]{2,1,0:T(8,128)(2,1)}, u32[]{:S(2)}, u32[]{:S(2)}) async-start(bf16[16,1024,128]{2,1,0:T(8,128)(2,1)} %broadcast_in_dim.50), calls=%async_computation.6 | async-start | bytes 8388608 | tf_op jit(solution)/shard_map/all_to_all | solution.py:27
  420.3 50.5 %all-to-all-done.6 = bf16[16,1024,128]{2,1,0:T(8,128)(2,1)} async-done(((bf16[16,1024,128]{2,1,0:T(8,128)(2,1)}), bf16[16,1024,128]{2,1,0:T(8,128)(2,1)}, u32[]{:S(2)}, u32[]{:S(2)}) %all-to-all-start.6) | async-done | bytes 4194336 | tf_op jit(solution)/shard_map/all_to_all | solution.py:27
  473.3 3.6 fusion.52
  476.9 5.7 collective-permute-start.11
  483.9 2.8 collective-permute-done.12
  489.1 3.1 collective-permute-done.13
  493.1 50.2 %all_to_all.62 = bf16[16,1024,128]{2,1,0:T(8,128)(2,1)S(1)} all-to-all(bf16[16,1024,128]{2,1,0:T(8,128)(2,1)S(1)} %broadcast_in_dim.51), channel_id=1, replica_groups=mesh['row'=8,'col'=16] {'col'}, dimensions={0} | all-to-all | bytes 8388608 | tf_op jit(solution)/shard_map/all_to_all | solution.py:27
  546.6 5.1 collective-permute-start.14
  558.2 3.1 collective-permute-done.16
  561.4 2.8 broadcast_in_dim.52
  564.2 4.5 all-to-all-start.8
  568.7 50.8 %all-to-all-done.8 = bf16[16,1024,128]{2,1,0:T(8,128)(2,1)} async-done(((bf16[16,1024,128]{2,1,0:T(8,128)(2,1)}), bf16[16,1024,128]{2,1,0:T(8,128)(2,1)}, u32[]{:S(2)}, u32[]{:S(2)}) %all-to-all-start.8) | async-done | bytes 4194336 | tf_op jit(solution)/shard_map/all_to_all | solution.py:27
  619.5 4.8 copy.25
  624.3 24.6 %gather_fusion.2 = bf16[8192,128]{1,0:T(8,128)(2,1)S(1)} fusion(bf16[16384,128]{1,0:T(8,128)(2,1)} %bitcast.80, s32[8192]{0:T(1024)S(1)} %broadcast_clamp_fusion), kind=kCustom, calls=%fused_computation.2 | custom fusion | bytes 4227072 | tf_op jit(solution)/shard_map/gather | solution.py:182
  651.2 5.7 collective-permute-start.17
  658.2 2.8 collective-permute-done.18
  661.5 29.3 %all_to_all.63 = bf16[16,512,128]{2,1,0:T(8,128)(2,1)S(1)} all-to-all(bf16[16,512,128]{2,1,0:T(8,128)(2,1)S(1)} %broadcast_in_dim.53), channel_id=1, replica_groups=mesh['row'=8,'col'=16] {'col'}, dimensions={0} | all-to-all | bytes 4194304 | tf_op jit(solution)/shard_map/all_to_all | solution.py:27
  693.4 3.3 collective-permute-start.19
  702.7 3.7 all-to-all-start.10
  706.4 25.8 %all-to-all-done.10 = bf16[16,512,128]{2,1,0:T(8,128)(2,1)S(1)} async-done(((bf16[16,512,128]{2,1,0:T(8,128)(2,1)}), bf16[16,512,128]{2,1,0:T(8,128)(2,1)S(1)}, u32[]{:S(2)}, u32[]{:S(2)}) %all-to-all-start.10) | async-done | bytes 2097184 | tf_op jit(solution)/shard_map/all_to_all | solution.py:27
  735.3 12.1 %gather_fusion.3 = bf16[4096,128]{1,0:T(8,128)(2,1)S(1)} fusion(bf16[8192,128]{1,0:T(8,128)(2,1)S(1)} %bitcast.82, s32[4096]{0:T(1024)S(1)} %broadcast_clamp_fusion.1), kind=kCustom, calls=%fused_computation.3 | custom fusion | bytes 2113536 | tf_op jit(solution)/shard_map/gather | solution.py:182
  749.1 5.0 collective-permute-start.21
  755.2 19.6 %all_to_all.64 = bf16[16,256,128]{2,1,0:T(8,128)(2,1)S(1)} all-to-all(bf16[16,256,128]{2,1,0:T(8,128)(2,1)S(1)} %broadcast_in_dim.55), channel_id=1, replica_groups=mesh['row'=8,'col'=16] {'col'}, dimensions={0} | all-to-all | bytes 2097152 | tf_op jit(solution)/shard_map/all_to_all | solution.py:27
  (122 shorter events, 84.4 us)
Async XLA Ops:
  2.6 17.9 %all-to-all-start = ((bf16[8,384,128]{2,1,0:T(8,128)(2,1)}), bf16[8,384,128]{2,1,0:T(8,128)(2,1)S(1)}, u32[]{:S(2)}, u32[]{:S(2)}) async-start(bf16[8,384,128]{2,1,0:T(8,128)(2,1)} %broadcast_in_dim.43), calls=%async_computation | async-start | bytes 1572864 | tf_op jit(solution)/shard_map/all_to_all | solution.py:27
  36.6 7.9 %copy-start.6 = (s32[384]{0:T(512)S(1)}, s32[384]{0:T(512)}, u32[]{:S(2)}) copy-start(s32[384]{0:T(512)} %param.13) | copy-start | bytes 4612
  36.6 48.6 %copy-start.4 = (f32[384,128]{1,0:T(8,128)S(1)}, f32[384,128]{1,0:T(8,128)}, u32[]{:S(2)}) copy-start(f32[384,128]{1,0:T(8,128)} %param.10) | copy-start | bytes 589828
  36.7 48.5 %all-to-all-start.1 = ((f32[16,384,128]{2,1,0:T(8,128)}), f32[16,384,128]{2,1,0:T(8,128)S(1)}, u32[]{:S(2)}, u32[]{:S(2)}) async-start(f32[16,384,128]{2,1,0:T(8,128)} %bitcast.5), calls=%async_computation.1 | async-start | bytes 6291456 | tf_op jit(solution)/shard_map/all_to_all | solution.py:15
  85.3 12.1 %copy-start.5 = (s32[2,16384]{1,0:T(2,128)S(1)}, s32[2,16384]{1,0:T(2,128)}, u32[]{:S(2)}) copy-start(s32[2,16384]{1,0:T(2,128)} %param.17) | copy-start | bytes 393220
  85.3 29.6 %copy-start = (f32[384,128]{1,0:T(8,128)}, f32[384,128]{1,0:T(8,128)S(1)}, u32[]{:S(2)}) copy-start(f32[384,128]{1,0:T(8,128)S(1)} %sub.35) | copy-start | bytes 589828
  86.5 4.5 collective-permute-start
  92.2 20.9 %all-to-all-start.2 = ((bf16[16,256,128]{2,1,0:T(8,128)(2,1)}), bf16[16,256,128]{2,1,0:T(8,128)(2,1)S(1)}, u32[]{:S(2)}, u32[]{:S(2)}) async-start(bf16[16,256,128]{2,1,0:T(8,128)(2,1)} %broadcast_in_dim.46), calls=%async_computation.2 | async-start | bytes 2097152 | tf_op jit(solution)/shard_map/all_to_all | solution.py:27
  145.7 21.7 %collective-permute-start.1 = (bf16[2,2048,128]{2,1,0:T(8,128)(2,1)S(1)}, bf16[2,2048,128]{2,1,0:T(8,128)(2,1)S(1)}, u32[]{:S(2)}, u32[]{:S(2)}) collective-permute-start(bf16[2,2048,128]{2,1,0:T(8,128)(2,1)S(1)} %bitcast.99), channel_id=1, source_target_pairs={{0,32},{32,0},{16,48},{48,16},{64,96},{96,64},{80,112},{112,80},{1... | collective-permute-start | bytes 3145736 | tf_op jit(solution)/shard_map/ppermute | solution.py:41
  167.7 5.5 collective-permute-start.2
  193.8 3.3 collective-permute-start.3
  197.1 3.2 collective-permute-start.4
  202.1 29.6 %all-to-all-start.4 = ((bf16[16,512,128]{2,1,0:T(8,128)(2,1)}), bf16[16,512,128]{2,1,0:T(8,128)(2,1)S(1)}, u32[]{:S(2)}, u32[]{:S(2)}) async-start(bf16[16,512,128]{2,1,0:T(8,128)(2,1)} %broadcast_in_dim.48), calls=%async_computation.4 | async-start | bytes 4194304 | tf_op jit(solution)/shard_map/all_to_all | solution.py:27
  231.8 2.6 copy-start.2
  294.6 43.8 %collective-permute-start.5 = (bf16[4,2048,128]{2,1,0:T(8,128)(2,1)S(1)}, bf16[4,2048,128]{2,1,0:T(8,128)(2,1)S(1)}, u32[]{:S(2)}, u32[]{:S(2)}) collective-permute-start(bf16[4,2048,128]{2,1,0:T(8,128)(2,1)S(1)} %bitcast.96), channel_id=1, source_target_pairs={{0,64},{64,0},{16,80},{80,16},{32,96},{96,32},{48,112},{112,48},{1... | collective-permute-start | bytes 6291464 | tf_op jit(solution)/shard_map/ppermute | solution.py:41
  339.0 21.5 %collective-permute-start.6 = (bf16[2,2048,128]{2,1,0:T(8,128)(2,1)S(1)}, bf16[2,2048,128]{2,1,0:T(8,128)(2,1)S(1)}, u32[]{:S(2)}, u32[]{:S(2)}) collective-permute-start(bf16[2,2048,128]{2,1,0:T(8,128)(2,1)S(1)} %select_convert_fusion.1), channel_id=1, source_target_pairs={{0,32},{32,0},{16,48},{48,16},{64,96},{96,64},{80,112},{112,80},{1... | collective-permute-start | bytes 3145736 | tf_op jit(solution)/shard_map/ppermute | solution.py:41
  360.9 6.5 collective-permute-start.7
  391.3 3.0 collective-permute-start.8
  394.4 3.2 collective-permute-start.9
  397.6 5.4 collective-permute-start.10
  405.9 64.9 %all-to-all-start.6 = ((bf16[16,1024,128]{2,1,0:T(8,128)(2,1)}), bf16[16,1024,128]{2,1,0:T(8,128)(2,1)}, u32[]{:S(2)}, u32[]{:S(2)}) async-start(bf16[16,1024,128]{2,1,0:T(8,128)(2,1)} %broadcast_in_dim.50), calls=%async_computation.6 | async-start | bytes 8388608 | tf_op jit(solution)/shard_map/all_to_all | solution.py:27
  476.9 6.6 collective-permute-start.11
  483.6 3.2 collective-permute-start.12
  486.8 5.4 collective-permute-start.13
  493.1 50.8 %slice-start = ((s8[7340032]{0:T(1024)(128)(4,1)}), s8[4194304]{0:T(1024)(128)(4,1)S(1)}, s32[]{:S(2)}) async-start(s8[7340032]{0:T(1024)(128)(4,1)} %bitcast.106), calls=%async_computation.12 | async-start | bytes 8388608
  543.3 1.9 slice-start.1
  546.6 6.0 collective-permute-start.14
  552.6 3.2 collective-permute-start.15
  555.9 5.4 collective-permute-start.16
  564.2 55.3 %all-to-all-start.8 = ((bf16[16,1024,128]{2,1,0:T(8,128)(2,1)}), bf16[16,1024,128]{2,1,0:T(8,128)(2,1)}, u32[]{:S(2)}, u32[]{:S(2)}) async-start(bf16[16,1024,128]{2,1,0:T(8,128)(2,1)} %broadcast_in_dim.52), calls=%async_computation.8 | async-start | bytes 8388608 | tf_op jit(solution)/shard_map/all_to_all | solution.py:27
  651.2 6.6 collective-permute-start.17
  657.9 3.2 collective-permute-start.18
  693.4 4.2 collective-permute-start.19
  697.7 3.2 collective-permute-start.20
  702.7 29.6 %all-to-all-start.10 = ((bf16[16,512,128]{2,1,0:T(8,128)(2,1)}), bf16[16,512,128]{2,1,0:T(8,128)(2,1)S(1)}, u32[]{:S(2)}, u32[]{:S(2)}) async-start(bf16[16,512,128]{2,1,0:T(8,128)(2,1)} %broadcast_in_dim.54), calls=%async_computation.10 | async-start | bytes 4194304 | tf_op jit(solution)/shard_map/all_to_all | solution.py:27
  732.2 1.3 copy-start.1
  749.1 5.9 collective-permute-start.21
  755.2 21.4 %copy-start.3 = (f32[384,128]{1,0:T(8,128)S(1)}, f32[384,128]{1,0:T(8,128)}, u32[]{:S(2)}) copy-start(f32[384,128]{1,0:T(8,128)} %param.9) | copy-start | bytes 589828
where the time goes:
time: 783 us; the launch traced here: 778 us
  waiting for transfers between devices  334 us (43%)
  blocking collectives  143 us (18%)
  starting transfers between devices  99.7 us (13%)
  other arithmetic  90.4 us (12%)
  local copies, waits for them, and re-layouts  79.3 us (10%)
  matrix products  29.8 us (4%)
    all_to_all x6, waiting for transfers between devices, sent_to_all(): return lax.all_to_all(copies, axis, split_axis=0, concat_axis=0, tiled=True)  180 us
    ppermute x22, waiting for transfers between devices, from_partner(): return lax.ppermute(block, axis, route)  114 us
    all_to_all x3, blocking collectives, sent_to_all(): return lax.all_to_all(copies, axis, split_axis=0, concat_axis=0, tiled=True)  99.1 us
    scatter-add x2, other arithmetic, front_reduce(): zeros_sum.at[targets].add(partials)  72.9 us
    ppermute x22, starting transfers between devices, from_partner(): return lax.ppermute(block, axis, route)  54.5 us
    all_to_all x2, blocking collectives, summed_on_arrival(): lax.all_to_all(blocks, axis, split_axis=0, concat_axis=0, tiled=True)  43.9 us
    all_to_all x1, waiting for transfers between devices, summed_on_arrival(): lax.all_to_all(blocks, axis, split_axis=0, concat_axis=0, tiled=True)  40.5 us
    all_to_all x6, starting transfers between devices, sent_to_all(): return lax.all_to_all(copies, axis, split_axis=0, concat_axis=0, tiled=True)  37.3 us
  transfers between devices with their start and end apart: 29, of which 29 were waited for; matrix products, arithmetic and copies ran while one was open for 1% of the time, Pallas kernels for 0%

commit v1 on v0

v1 whole, which is shorter than its diff:
```python
import functools
import math

import jax
import jax.numpy as jnp
from jax import lax
from jax.experimental import pallas as pl
from jax.experimental.pallas import tpu as pltpu
from jax.sharding import PartitionSpec as P

MESH = pl.DeviceIdType.MESH
BF = jnp.bfloat16
F32 = jnp.float32
CORES = 2
SETS = 11


def sent_to_all(x, axis):
    copies = jnp.broadcast_to(x, (lax.axis_size(axis), *x.shape))
    return lax.all_to_all(copies, axis, split_axis=0, concat_axis=0, tiled=True)


def dot(a, b):
    return jnp.dot(a, b, preferred_element_type=F32)


def place_kernel(levels, spans, lower_ref, *refs):
    targets, out_ref, wide, placed = refs[:levels], refs[levels], refs[levels + 1], refs[levels + 2]
    tile = 256
    total = lower_ref.shape[0]

    @pl.loop(0, total // tile)
    def _(i):
        at = pl.ds(pl.multiple_of(i * tile, tile), tile)
        wide[at, :] = lower_ref[at, :].astype(F32)

    @pl.loop(0, 2 * total // tile)
    def _(i):
        at = pl.ds(pl.multiple_of(i * tile, tile), tile)
        placed[at, :] = jnp.zeros((tile, wide.shape[1]), F32)

    start = 0
    for level in range(levels):
        span = spans[level]
        step = 16

        @pl.loop(0, span // step)
        def _(i, level=level, start=start):
            for j in range(step):
                u = i * step + j
                to = targets[level][u]
                placed[pl.ds(2 * start + to, 1), :] = wide[pl.ds(start + u, 1), :]

        start += span

    rows = out_ref.shape[1]

    @pl.loop(0, out_ref.shape[0])
    def _(i):
        out_ref[i] = placed[pl.ds(pl.multiple_of(i * rows, rows), rows), :].astype(BF)


def place_rows(lower, targets):
    total, width = lower.shape
    spans = [t.shape[0] for t in targets]
    levels = len(spans)
    blocks = 2 * total // 128
    vmem = pl.BlockSpec(memory_space=pltpu.VMEM)
    smem = pl.BlockSpec(memory_space=pltpu.SMEM)
    return pl.pallas_call(
        functools.partial(place_kernel, levels, spans),
        out_shape=jax.ShapeDtypeStruct((blocks, 128, width), BF),
        in_specs=[vmem] + [smem] * levels,
        out_specs=vmem,
        scratch_shapes=[pltpu.VMEM((total, width), F32), pltpu.VMEM((2 * total, width), F32)],
        compiler_params=pltpu.CompilerParams(vmem_limit_bytes=56 * 2**20),
        cost_estimate=pl.CostEstimate(flops=10**10, bytes_accessed=10**7, transcendentals=0),
        name="place_rows",
    )(lower, *targets)


class Comm:
    def __init__(self, sizes, rows):
        self.axes = [a for a in ("x", "y", "z") if sizes[a] > 1]
        self.n = {a: sizes[a] for a in self.axes}
        if len(self.axes) == 2:
            a, b = self.axes
            half = rows // 2
            self.parts = [((a, b), 0, half), ((b, a), half, half)]
        else:
            third = rows * 3 // 8
            last = rows - 2 * third
            self.parts = [
                (("x", "y", "z"), 0, third),
                (("z", "x", "y"), third, third),
                (("y", "z", "x"), 2 * third, last),
            ]
        self.rows = rows

    def sum_parts(self):
        if len(self.axes) == 2:
            return self.parts
        third = self.rows * 3 // 8
        last = self.rows - 2 * third
        return [
            (("y", "z", "x"), 0, third),
            (("z", "x", "y"), third, third),
            (("x", "y", "z"), 2 * third, last),
        ]

    def sum_scratch(self):
        shapes = []
        for order, _, rows in self.sum_parts():
            left = list(self.axes)
            for j, a in enumerate(order):
                left.remove(a)
                dims = tuple(self.n[b] for b in left)
                shapes.append(pltpu.VMEM((self.n[a] - 1, *dims, rows, 128), BF))
                if j + 1 < len(order):
                    shapes.append(pltpu.VMEM((*dims, rows, 128), BF))
        return shapes


def main_kernel(cfg, *refs):
    names = cfg["names"]
    r = dict(zip(names, refs))
    levels, groups0, ny, nz, seg = cfg["levels"], cfg["groups0"], cfg["ny"], cfg["nz"], cfg["seg"]
    comms, comm_b = cfg["comms"], cfg["comm_b"]
    row = lax.axis_index("row")
    col = lax.axis_index("col")
    core = row % CORES
    other = 1 - core
    coord = {"x": row // CORES, "y": col // nz, "z": col % nz}
    size = {"x": cfg["nx"], "y": ny, "z": nz}
    plane = ny * nz * seg

    def device(axis, d, n):
        here = coord[axis]
        if axis == "x":
            base = here // n * n
            there = base + (here - base + d) % n
            return (there * CORES + core, col)
        there = (here + d) % n
        if axis == "y":
            return (row, there * nz + coord["z"])
        return (row, coord["y"] * nz + there)

    partner = (row + 1 - 2 * core, col)

    barrier = pltpu.get_barrier_semaphore()
    peers = [partner]
    for a in ("x", "y", "z"):
        peers += [device(a, d, size[a]) for d in range(1, size[a])]
    for peer in peers:
        pl.semaphore_signal(barrier, inc=1, device_id=peer, device_id_type=MESH)

    load = r["load_sem"]
    get_a = pltpu.make_async_copy(r["blocks"], r["al"], load.at[0])
    get_a.start()
    get_p = pltpu.make_async_copy(r["tri"], r["tri_buf"], load.at[1])
    get_p.start()
    get_w = pltpu.make_async_copy(r["upper"], r["upper_buf"], load.at[2])
    get_w.start()

    per = r["rhs"].shape[0]
    lanes = lax.broadcasted_iota(jnp.int32, (per, per), 1)
    r["hot"][...] = jnp.where(lanes == r["order"][...], 1.0, 0.0).astype(BF)

    pl.semaphore_wait(barrier, len(peers))

    def remote(src, dst, s, t, to):
        return pltpu.make_async_remote_copy(
            src_ref=src, dst_ref=dst, send_sem=s, recv_sem=t, device_id=to, device_id_type=MESH
        )

    def reduce(comm, first, scratch, turn):
        bufs = iter(scratch)
        state = []
        for order, r0, rows in comm.sum_parts():
            state.append(dict(order=order, r0=r0, rows=rows, left=list(comm.axes), cur=None))
        local = {a: coord[a] % comm.n[a] for a in comm.axes}
        stages = []
        for p, st in enumerate(state):
            mine = []
            for j in range(len(st["order"])):
                recv = next(bufs)
                nxt = next(bufs) if j + 1 < len(st["order"]) else None
                mine.append((recv, nxt))
            stages.append(mine)
        out = [None] * len(state)
        steps = len(state[0]["order"])

        def region(st, idx):
            if st["cur"] is None:
                return first(idx, pl.ds(st["r0"], st["rows"]))
            return st["cur"].at[tuple(idx)]

        def begin(p, j):
            st = state[p]
            a = st["order"][j]
            n = comm.n[a]
            pos = st["left"].index(a)
            copies = []
            for d in range(1, n):
                idx = [slice(None)] * len(st["left"])
                idx[pos] = (local[a] + d) % n
                c = remote(
                    region(st, idx),
                    stages[p][j][0].at[d - 1],
                    r["send_sem"].at[p, j, d - 1],
                    r["recv_sem"].at[turn, p, j, d - 1],
                    device(a, d, n),
                )
                c.start()
                copies.append(c)
            st["copies"] = copies

        def finish(p, j):
            st = state[p]
            a = st["order"][j]
            n = comm.n[a]
            pos = st["left"].index(a)
            for c in st["copies"]:
                c.wait_recv()
            recv, nxt = stages[p][j]
            rest = [b for b in st["left"] if b != a]
            dims = [comm.n[b] for b in rest]
            count = math.prod(dims)

            def total(at):
                idx = list(at)
                idx.insert(pos, local[a])
                value = region(st, idx)[...].astype(F32)
                for d in range(1, n):
                    value = value + recv[(d - 1, *at)].astype(F32)
                return value

            if nxt is None:
                out[p] = total([])
            elif len(dims) == 1:
                for i in range(dims[0]):
                    nxt[i] = total([i]).astype(BF)
            else:

                @pl.loop(0, count)
                def _(i):
                    at = [i // dims[1], i % dims[1]]
                    nxt[at[0], at[1]] = total(at).astype(BF)

            for c in st["copies"]:
                c.wait_send()
            st["left"] = rest
            st["cur"] = nxt

        for p in range(len(state)):
            begin(p, 0)
        for j in range(steps):
            for p in range(len(state)):
                finish(p, j)
                if j + 1 < steps:
                    begin(p, j + 1)
        return [(st["r0"], st["rows"], out[p]) for p, st in enumerate(state)]

    def gather(level, value, buf, turn):
        comm = comms[level]
        local = {a: coord[a] % comm.n[a] for a in comm.axes}
        here = {"x": local.get("x", 0), "y": coord["y"], "z": coord["z"]}

        def block(idx, c, rows):
            return buf.at[(idx["x"], c, idx["y"], idx["z"], rows)]

        every = pl.ds(0, seg)
        buf[here["x"], core, here["y"], here["z"]] = value
        d2d_send = r["d2d_send"].at[0]
        d2d_recv = r["d2d_recv"].at[turn]
        own = block(here, core, every)
        remote(own, own, d2d_send, d2d_recv, partner).start()
        pending = []

        def span(order, j, shift_axis=None, d=0):
            idx = dict(here)
            for a in order[:j]:
                idx[a] = slice(None)
            if shift_axis is not None:
                n = comm.n[shift_axis]
                idx[shift_axis] = (local[shift_axis] + n - d) % n
            return idx

        def begin(p, j):
            order, r0, rows = comm.parts[p]
            a = order[j]
            n = comm.n[a]
            src = block(span(order, j), core, pl.ds(r0, rows))
            for d in range(1, n):
                c = remote(
                    src,
                    src,
                    r["send_sem"].at[p, j, d - 1],
                    r["recv_sem"].at[turn, p, j, d - 1],
                    device(a, d, n),
                )
                c.start()
                pending.append(c)

        def finish(p, j):
            order, r0, rows = comm.parts[p]
            a = order[j]
            n = comm.n[a]
            for d in range(1, n):
                got = block(span(order, j, a, d), core, pl.ds(r0, rows))
                remote(
                    got,
                    got,
                    r["send_sem"].at[p, j, d - 1],
                    r["recv_sem"].at[turn, p, j, d - 1],
                    device(a, d, n),
                ).wait_recv()
                remote(got, got, d2d_send, d2d_recv, partner).start()

        steps = len(comm.axes)
        for p in range(len(comm.parts)):
            begin(p, 0)
        for j in range(steps):
            for p in range(len(comm.parts)):
                finish(p, j)
                if j + 1 < steps:
                    begin(p, j + 1)
        for c in pending:
            c.wait_send()
        mine, theirs = buf.at[:, core], buf.at[:, other]
        remote(mine, theirs, d2d_send, d2d_recv, partner).wait()

    offsets = cfg["offsets"]

    def triangle(level, buf, lower):
        off = offsets[level]
        fronts = groups0 * 2**level
        me = row % fronts

        def panel(g):
            return r["tri_buf"][:, pl.ds(pl.multiple_of(off + g * plane, 128), plane)]

        def vector(g):
            return buf[g // CORES, g % CORES].reshape(plane, 128)

        row_ids = col * seg + lax.broadcasted_iota(jnp.int32, (seg, plane), 0)
        col_ids = lax.broadcasted_iota(jnp.int32, (seg, plane), 1)
        keep = col_ids < row_ids if lower else col_ids >= row_ids
        masked = jnp.where(keep, panel(me).astype(F32), 0.0).astype(BF)
        acc = dot(masked, vector(me))

        def more(g, acc):
            return acc + dot(panel(g), vector(g))

        if lower:
            return lax.fori_loop(0, me, more, acc)
        return lax.fori_loop(me + 1, fronts, more, acc)

    get_a.wait()
    al, sol, tb = r["al"], r["gathered"], r["tb"]
    kb = cfg["kb"]
    bpd = per // 128

    @pl.loop(0, ny * nz)
    def _(c):
        for j in range(bpd):
            i = c * bpd + j
            left = jnp.concatenate([al[i * kb + s] for s in range(kb)], 1)
            right = jnp.concatenate(
                [sol[r["where"][i * kb + s]] for s in range(kb)], 0
            )
            tb[c // nz, c % nz, j * 128 : (j + 1) * 128, :] = dot(left, right).astype(BF)

    get_l = pltpu.make_async_copy(r["placed"], al, load.at[0])
    get_l.start()

    def first_b(idx, rows):
        return tb.at[(*idx, rows)]

    for r0, rows, value in reduce(comm_b, first_b, r["sum_b"], 0):
        at = slice(r0, r0 + rows)
        res = r["rhs"][at, :] - value
        r["residual"][at, :] = res
        hi = res.astype(BF)
        r["split"][at, 0:128] = hi
        r["split"][at, 128:256] = (res - hi.astype(F32)).astype(BF)
    both = dot(r["hot"][...], r["split"][...])
    r["vee"][...] = both[:, 0:128] + both[:, 128:256]

    get_p.wait()
    turn = 1
    buf_a, buf_b = r["buf_a"], r["buf_b"]
    incoming = None
    for level in range(levels):
        e = r["vee"][level * seg : (level + 1) * seg, :]
        if level > 0:
            parts = incoming
            for r0, rows, value in parts:
                r["minus"][r0 : r0 + rows, :] = value
            e = e - r["minus"][...]
        cb = e.astype(BF)
        gather(level, cb, buf_a[level], turn % SETS)
        turn += 1
        y = (triangle(level, buf_a[level], True) + cb.astype(F32)).astype(BF)
        r["why"][level] = y
        if level == 0:
            get_l.wait()
        if level + 1 < levels:
            t, rd = r["t"][level], r["rd"][level]
            nx = t.shape[0]
            base = 2 * offsets[level] // 128
            half = ny // 2
            per_half = half * nz

            def update(xi, ci, level=level, t=t, base=base, y=y):
                for h in range(2):
                    at = base + (xi * CORES + ci) * (ny * nz) + h * per_half
                    block = al[pl.ds(at, per_half)].reshape(per_half * 128, 128)
                    res = dot(block, y).astype(BF)
                    t[xi, ci, h * half : (h + 1) * half] = res.reshape(half, nz, 128, 128)

            d2d_send, d2d_recv = r["d2d_send"].at[0], r["d2d_recv"].at[turn % SETS]
            for xi in range(nx):
                update(xi, other)
                remote(t.at[xi, other], rd.at[xi], d2d_send, d2d_recv, partner).start()
            for xi in range(nx):
                update(xi, core)
            remote(t.at[:, other], rd, d2d_send, d2d_recv, partner).wait()

            @pl.loop(0, nx * ny)
            def _(i, t=t, rd=rd):
                xi, yi = i // ny, i % ny
                for zi in range(nz):
                    value = t[xi, core, yi, zi].astype(F32) + rd[xi, yi, zi].astype(F32)
                    t[xi, core, yi, zi] = value.astype(BF)

            def first(idx, rows, t=t):
                return t.at[(idx[0], core, idx[1], idx[2], rows)]

            incoming = reduce(comms[level + 1], first, r["sums"][level], turn % SETS)
            turn += 1

    get_w.wait()
    xb = None
    for level in reversed(range(levels)):
        z = r["why"][level]
        if level + 1 < levels:
            src = buf_a[level + 1]
            wide, picked = r["wide"], r["picked"]
            xs = src.shape[0]

            @pl.loop(0, xs * CORES * ny)
            def _(i, src=src):
                xi, ci, yi = i // (CORES * ny), i // ny % CORES, i % ny
                block = src[xi, ci, yi].reshape(nz * 128, 128)
                wide[pl.ds(pl.multiple_of(i * nz * 128, 128), nz * 128), :] = block.astype(F32)

            m = offsets[level + 1] - offsets[level]
            tile = picked.shape[0]
            where = r["targets"][level]
            step = 16

            def chunk(i, acc, level=level, where=where):
                @pl.loop(0, tile // step)
                def _(u):
                    for v in range(step):
                        w = u * step + v
                        picked[w] = wide[where[i * tile + w]]

                at = pl.ds(pl.multiple_of(offsets[level] + i * tile, 128), tile)
                return acc + dot(r["upper_buf"][:, at], picked[...].astype(BF))

            total = lax.fori_loop(0, m // tile, chunk, jnp.zeros((seg, 128), F32))
            z = (z.astype(F32) - total).astype(BF)
        gather(level, z, buf_b[level], turn % SETS)
        turn += 1
        x = triangle(level, buf_b[level], False)
        at = slice(level * seg, (level + 1) * seg)
        r["refined"][at, :] = r["old"][at, :] + x
        if level > 0:
            gather(level, x.astype(BF), buf_a[level], turn % SETS)
            turn += 1


def refine(nx, ny, nz, gathered, solution, rhs, blocks, where, order, tri, placed, upper, targets):
    per = rhs.shape[0]
    levels = len(targets) + 1
    seg = per // levels
    cols = ny * nz
    groups0 = CORES
    span0 = groups0 * cols * seg
    offsets = [span0 * (2**k - 1) for k in range(levels + 1)]
    comms = [Comm({"x": 2**k, "y": ny, "z": nz}, seg) for k in range(levels)]
    comm_b = Comm({"x": 1, "y": ny, "z": nz}, per)
    vmem = pl.BlockSpec(memory_space=pltpu.VMEM)
    smem = pl.BlockSpec(memory_space=pltpu.SMEM)
    hbm = pl.BlockSpec(memory_space=pl.ANY)
    ins = [
        ("gathered", vmem), ("old", vmem), ("rhs", vmem), ("blocks", hbm), ("where", smem), ("order", vmem),
        ("tri", hbm), ("placed", hbm), ("upper", hbm),
    ]
    names = [n for n, _ in ins] + [f"target{k}" for k in range(levels - 1)]
    in_specs = [s for _, s in ins] + [smem] * (levels - 1)
    names += ["refined", "residual"]
    front = lambda k: (2**k, CORES, ny, nz, seg, 128)
    scratch = {
        "al": pltpu.VMEM(blocks.shape, BF),
        "tri_buf": pltpu.VMEM(tri.shape, BF),
        "upper_buf": pltpu.VMEM(upper.shape, BF),
        "hot": pltpu.VMEM((per, per), BF),
        "tb": pltpu.VMEM((ny, nz, per, 128), BF),
        "split": pltpu.VMEM((per, 256), BF),
        "vee": pltpu.VMEM((per, 128), F32),
        "minus": pltpu.VMEM((seg, 128), F32),
        "why": pltpu.VMEM((levels, seg, 128), BF),
        "wide": pltpu.VMEM((2 ** (levels - 1) * span0, 128), F32),
        "picked": pltpu.VMEM((1024, 128), F32),
        "load_sem": pltpu.SemaphoreType.DMA((3,)),
        "send_sem": pltpu.SemaphoreType.DMA((3, 3, 3)),
        "recv_sem": pltpu.SemaphoreType.DMA((SETS, 3, 3, 3)),
        "d2d_send": pltpu.SemaphoreType.DMA((1,)),
        "d2d_recv": pltpu.SemaphoreType.DMA((SETS,)),
    }
    names += list(scratch)
    shapes = list(scratch.values())
    lists = {
        "buf_a": [pltpu.VMEM(front(k), BF) for k in range(levels)],
        "buf_b": [pltpu.VMEM(front(k), BF) for k in range(levels)],
        "t": [pltpu.VMEM(front(k + 1), BF) for k in range(levels - 1)],
        "rd": [pltpu.VMEM((2 ** (k + 1), ny, nz, seg, 128), BF) for k in range(levels - 1)],
        "sum_b": comm_b.sum_scratch(),
    }
    for k in range(levels - 1):
        lists[f"sums{k}"] = comms[k + 1].sum_scratch()
    for name, items in lists.items():
        names += [f"{name}.{i}" for i in range(len(items))]
        shapes += items

    def body(*refs):
        flat = dict(zip(names, refs))
        r = {n: v for n, v in flat.items() if "." not in n}
        for name, items in lists.items():
            r[name] = [flat[f"{name}.{i}"] for i in range(len(items))]
        r["sums"] = [r[f"sums{k}"] for k in range(levels - 1)]
        r["targets"] = [r[f"target{k}"] for k in range(levels - 1)]
        cfg = dict(
            names=list(r), levels=levels, groups0=groups0, nx=nx, ny=ny, nz=nz, seg=seg,
            comms=comms, comm_b=comm_b, offsets=offsets, kb=where.shape[0] // (cols * per // 128),
        )
        main_kernel(cfg, *r.values())

    return pl.pallas_call(
        body,
        out_shape=(jax.ShapeDtypeStruct(rhs.shape, F32), jax.ShapeDtypeStruct(rhs.shape, F32)),
        in_specs=in_specs,
        out_specs=(vmem, vmem),
        scratch_shapes=shapes,
        compiler_params=pltpu.CompilerParams(
            collective_id=0, has_side_effects=True, vmem_limit_bytes=67043328
        ),
        cost_estimate=pl.CostEstimate(flops=10**10, bytes_accessed=3 * 10**7, transcendentals=0),
        name="refine_step",
    )(gathered, solution, rhs, blocks, where, order, tri, placed, upper, *targets)


def on_device(
    solution,
    right_side,
    block_values,
    block_columns,
    row_order,
    tri_inverses,
    lower_updates,
    upper_updates,
    update_rows,
):
    row_count = lax.axis_size("row")
    col_count = lax.axis_size("col")
    levels = row_count.bit_length() - 1
    per = solution.shape[0]
    seg = per // levels
    block_size = block_values.shape[2]
    per_block = per // block_size
    row_index = lax.axis_index("row")
    col_index = lax.axis_index("col")
    span0 = CORES * col_count * seg
    gathered = sent_to_all(solution.astype(BF), "row").reshape(row_count * per_block, block_size, -1)
    targets = []
    for k in range(levels - 1):
        span = span0 * 2**k
        front = row_index // 2 ** (k + 1)
        targets.append(lax.dynamic_slice_in_dim(update_rows[k], front * span, span))
    placed = place_rows(lower_updates, targets)
    local_block = block_columns // (per_block * col_count) * per_block + block_columns % per_block
    order = row_order - (row_index * col_count + col_index) * per
    ny = math.isqrt(col_count)
    return refine(
        row_count // CORES,
        ny,
        col_count // ny,
        gathered,
        solution,
        right_side,
        block_values.reshape(-1, block_size, block_size),
        local_block.reshape(-1),
        order.reshape(-1, 1),
        tri_inverses,
        placed,
        upper_updates,
        targets,
    )


def solution(mesh):
    in_specs = (
        P(("row", "col"), None),
        P(("row", "col"), None),
        P("row", "col", None, None),
        P("row", "col"),
        P(("row", "col")),
        P(("row", "col"), None),
        P(None, ("row", "col")),
        P(("row", "col"), None),
        P(),
    )
    out_specs = (P(("row", "col"), None), P(("row", "col"), None))
    return jax.shard_map(
        on_device, mesh=mesh, in_specs=in_specs, out_specs=out_specs, check_vma=False
    )
```

time: 783 us -> 266 us (0.34)
  waiting for transfers between devices: 334 us -> 0.01 us
  Pallas kernels: 0 us -> 249 us
  blocking collectives: 143 us -> 0 us
  starting transfers between devices: 99.7 us -> 5.79 us
  other arithmetic: 90.4 us -> 2.32 us
  local copies, waits for them, and re-layouts: 79.3 us -> 8.04 us
  matrix products: 29.8 us -> 0 us
    pallas_call x0 -> x2, Pallas kernels: none -> 249 us  [the longest x1 228 us: refine(): pl.pallas_call(body, out_shape=(jax.ShapeDtypeStruct(rhs.shape, F32), jax...]
    all_to_all x6 -> x1, waiting for transfers between devices: 180 us -> 0.01 us  [sent_to_all(): return lax.all_to_all(copies, axis, split_axis=0, concat_axis=0, tiled=True)]
    all_to_all x5 -> x0, blocking collectives: 143 us -> none  [the longest x3 99.1 us: sent_to_all(): return lax.all_to_all(copies, axis, split_axis=0, concat_axis=0, tiled=True)]
    ppermute x22 -> x0, waiting for transfers between devices: 114 us -> none  [from_partner(): return lax.ppermute(block, axis, route)]
    scatter-add x2 -> x0, other arithmetic: 72.9 us -> none  [front_reduce(): zeros_sum.at[targets].add(partials)]
    ppermute x22 -> x0, starting transfers between devices: 54.5 us -> none  [from_partner(): return lax.ppermute(block, axis, route)]
    gather x4 -> x0, local copies, waits for them, and re-layouts: 45.9 us -> none  [the longest x2 36.8 us: on_device(): picked_rows = parent_full[targets_all[depth_k]]]
    all_to_all x1 -> x0, waiting for transfers between devices: 40.5 us -> none  [summed_on_arrival(): lax.all_to_all(blocks, axis, split_axis=0, concat_axis=0, tiled=True)]
  transfers between devices with their start and end apart: 29 -> 1, of which waited for: 29 -> 0; matrix products, arithmetic and copies ran while one was open for 1% -> 2% of each run, Pallas kernels for 0% -> 8%
where the time goes in v1:
time: 266 us
  Pallas kernels  249 us (94%)
  local copies, waits for them, and re-layouts  8.04 us (3%)
  starting transfers between devices  5.79 us (2%)
    pallas_call x1, Pallas kernels, refine(): pl.pallas_call(body, out_shape=(jax.ShapeDtypeStruct(rhs.shape, F32), jax...  228 us
    pallas_call x1, Pallas kernels, place_rows(): pl.pallas_call(functools.partial(place_kernel, levels, spans), out_shape=...  20.9 us
    all_to_all x1, starting transfers between devices, sent_to_all(): return lax.all_to_all(copies, axis, split_axis=0, concat_axis=0, tiled=True)  5.79 us
  transfers between devices with their start and end apart: 1, of which 0 were waited for; matrix products, arithmetic and copies ran while one was open for 2% of the time, Pallas kernels for 8%

profile of v1, /device:TPU:1, one launch (start us, length us, event | category | flops | bytes accessed | tf_op | source)
XLA Modules:
  0.0 265.6 jit_solution(2494697817259084609)
XLA Ops:
  0.6 0.9 convert_element_type.3
  1.6 1.0 broadcast_in_dim.3
  2.6 5.8 %all-to-all-start = ((bf16[8,384,128]{2,1,0:T(8,128)(2,1)}), bf16[8,384,128]{2,1,0:T(8,128)(2,1)}, u32[]{:S(2)}, u32[]{:S(2)}) async-start(bf16[8,384,128]{2,1,0:T(8,128)(2,1)} %broadcast_in_dim.3), calls=%async_computation | async-start | bytes 1572864 | tf_op jit(solution)/shard_map/all_to_all | solution.py:20
  8.3 0.7 fusion
  9.0 0.1 copy.11
  9.1 0.6 reshape.20.refs_4_
  9.8 1.1 fusion.2
  10.9 0.7 broadcast_subtract_fusion
  11.6 0.8 reshape.22.refs_5_
  12.3 0.6 constant_dynamic-slice_fusion
  13.0 0.6 constant_dynamic-slice_fusion.1
  13.6 20.9 %place_rows.1.refs_7_ = bf16[192,128,128]{2,1,0:T(8,128)(2,1)} custom-call(bf16[12288,128]{1,0:T(8,128)(2,1)} %lower_ref.1, s32[4096]{0:T(1024)} %bitcast.6, s32[8192]{0:T(1024)} %bitcast.4), custom_call_target="tpu_custom_call" | custom-call | flops 10000000000 | bytes 10000000 | tf_op jit(solution)/shard_map/place_rows/pallas_call | solution.py:70
  34.4 0.0 all-to-all-done
  34.4 227.9 %refine_step.1 = (f32[384,128]{1,0:T(8,128)}, f32[384,128]{1,0:T(8,128)}) custom-call(bf16[24,128,128]{2,1,0:T(8,128)(2,1)} %bitcast.refs_0_, f32[384,128]{1,0:T(8,128)} %refs_1_.1, f32[384,128]{1,0:T(8,128)} %refs_2_.1, bf16[192,128,128]{2,1,0:T(8,128)(2,1)} %bitcast.8, s32[192]{0:T(256)} %reshape.20.refs_4_, s32[384,1]{1,0:T(8,128)} %reshape.22.refs_5_, ...), custom_call_target="tpu_custom_call" | custom-call | flops 10000000000 | bytes 30000000 | tf_op jit(solution)/shard_map/refine_step/pallas_call | solution.py:552
  262.3 1.6 copy.15
  263.9 1.6 copy.16
Async XLA Ops:
  2.6 31.9 %all-to-all-start = ((bf16[8,384,128]{2,1,0:T(8,128)(2,1)}), bf16[8,384,128]{2,1,0:T(8,128)(2,1)}, u32[]{:S(2)}, u32[]{:S(2)}) async-start(bf16[8,384,128]{2,1,0:T(8,128)(2,1)} %broadcast_in_dim.3), calls=%async_computation | async-start | bytes 1572864 | tf_op jit(solution)/shard_map/all_to_all | solution.py:20

commit v2 on v1

v2 whole, which is shorter than its diff:
```python
import functools
import math

import jax
import jax.numpy as jnp
from jax import lax
from jax.experimental import pallas as pl
from jax.experimental.pallas import tpu as pltpu
from jax.sharding import PartitionSpec as P

MESH = pl.DeviceIdType.MESH
BF = jnp.bfloat16
F32 = jnp.float32
CORES = 2


def sent_to_all(x, axis):
    copies = jnp.broadcast_to(x, (lax.axis_size(axis), *x.shape))
    return lax.all_to_all(copies, axis, split_axis=0, concat_axis=0, tiled=True)


def dot(a, b):
    return jnp.dot(a, b, preferred_element_type=F32)


def place_kernel(spans, lower, updates, out, narrow, wide, placed, done, where, sem_in, sem_out, sem_idx):
    rows = 256
    step = 32
    row = lax.axis_index("row")
    copies = []
    start = 0
    for level, span in enumerate(spans):
        at = pl.ds(start, span)
        front = pl.multiple_of(level * (updates.shape[0] // len(spans)) + row // 2 ** (level + 1) * span, 1024)
        idx = pltpu.make_async_copy(updates.at[pl.ds(front, span)], where.at[at], sem_idx.at[level])
        idx.start()
        got = pltpu.make_async_copy(lower.at[at], narrow.at[at], sem_in.at[level])
        got.start()
        copies.append((idx, got))
        start += span

    start = 0
    puts = []
    for level, span in enumerate(spans):

        @pl.loop(0, 2 * span // rows)
        def _(i, start=start):
            at = pl.multiple_of(2 * start + i * rows, rows)
            placed[pl.ds(at, rows), :] = jnp.zeros((rows, placed.shape[1]), F32)

        for copy in copies[level]:
            copy.wait()

        @pl.loop(0, span // rows)
        def _(i, start=start):
            at = pl.ds(pl.multiple_of(start + i * rows, rows), rows)
            wide[at, :] = narrow[at, :].astype(F32)

        @pl.loop(0, span // step)
        def _(i, start=start):
            for j in range(step):
                u = start + i * step + j
                placed[2 * start + where[u]] = wide[u]

        block = out.shape[1]
        for part in range(2):
            first = (2 * start + part * span) // block

            @pl.loop(first, first + span // block)
            def _(i):
                done[i] = placed[pl.ds(pl.multiple_of(i * block, block), block), :].astype(BF)

            at = pl.ds(first, span // block)
            put = pltpu.make_async_copy(done.at[at], out.at[at], sem_out.at[level, part])
            put.start()
            puts.append(put)
        start += span
    for put in puts:
        put.wait()


def place_rows(lower, updates, spans):
    total, width = lower.shape
    blocks = 2 * total // 128
    hbm = pl.BlockSpec(memory_space=pl.ANY)
    return pl.pallas_call(
        functools.partial(place_kernel, spans),
        out_shape=jax.ShapeDtypeStruct((blocks, 128, width), BF),
        in_specs=[hbm, hbm],
        out_specs=hbm,
        scratch_shapes=[
            pltpu.VMEM((total, width), BF),
            pltpu.VMEM((total, width), F32),
            pltpu.VMEM((2 * total, width), F32),
            pltpu.VMEM((blocks, 128, width), BF),
            pltpu.SMEM((total,), jnp.int32),
            pltpu.SemaphoreType.DMA((len(spans),)),
            pltpu.SemaphoreType.DMA((len(spans), 2)),
            pltpu.SemaphoreType.DMA((len(spans),)),
        ],
        compiler_params=pltpu.CompilerParams(vmem_limit_bytes=56 * 2**20),
        cost_estimate=pl.CostEstimate(flops=10**10, bytes_accessed=10**7, transcendentals=0),
        name="place_rows",
    )(lower, updates)


class Comm:
    def __init__(self, sizes, rows):
        self.axes = [a for a in ("x", "y", "z") if sizes[a] > 1]
        self.n = {a: sizes[a] for a in self.axes}
        if len(self.axes) == 2:
            a, b = self.axes
            half = rows // 2
            self.parts = [((a, b), 0, half), ((b, a), half, half)]
        else:
            third = rows * 3 // 8
            self.parts = [
                (("x", "y", "z"), 0, third),
                (("z", "x", "y"), third, third),
                (("y", "z", "x"), 2 * third, rows - 2 * third),
            ]
        self.rows = rows
        steps = len(self.axes)
        self.messages = [(j, mask) for j in range(steps) for mask in range(2**j)]
        self.blocks = math.prod(self.n.values())

    def span(self, order, mask, at):
        index = {}
        for i, a in enumerate(order):
            index[a] = slice(1, self.n[a]) if mask >> i & 1 else at.get(a, 0)
        return index

    def sum_scratch(self):
        shapes = []
        for order, _, rows in self.parts:
            for j, mask in self.messages:
                dims = [self.n[a] - 1 for a in self.axes if mask >> order.index(a) & 1]
                shapes.append(pltpu.VMEM((self.n[order[j]] - 1, *dims, rows, 128), BF))
        return shapes


def main_kernel(cfg, *refs):
    names = cfg["names"]
    r = dict(zip(names, refs))
    levels, groups0, ny, nz, seg = cfg["levels"], cfg["groups0"], cfg["ny"], cfg["nz"], cfg["seg"]
    comms, comm_b = cfg["comms"], cfg["comm_b"]
    row = lax.axis_index("row")
    col = lax.axis_index("col")
    core = row % CORES
    other = 1 - core
    coord = {"x": row // CORES, "y": col // nz, "z": col % nz}
    size = {"x": cfg["nx"], "y": ny, "z": nz}
    plane = ny * nz * seg

    def device(axis, d, n):
        here = coord[axis]
        if axis == "x":
            base = here // n * n
            there = base + (here - base + d) % n
            return (there * CORES + core, col)
        there = (here + d) % n
        if axis == "y":
            return (row, there * nz + coord["z"])
        return (row, coord["y"] * nz + there)

    partner = (row + 1 - 2 * core, col)

    barrier = pltpu.get_barrier_semaphore()
    peers = [partner]
    for a in ("x", "y", "z"):
        peers += [device(a, d, size[a]) for d in range(1, size[a])]
    for peer in peers:
        pl.semaphore_signal(barrier, inc=1, device_id=peer, device_id_type=MESH)

    load = r["load_sem"]
    get_a = pltpu.make_async_copy(r["blocks"], r["al"], load.at[0])
    get_a.start()
    get_p = pltpu.make_async_copy(r["tri"], r["tri_buf"], load.at[1])
    get_w = pltpu.make_async_copy(r["upper"], r["upper_buf"], load.at[2])

    per = r["rhs"].shape[0]
    source = lax.broadcasted_iota(jnp.int32, (per, per), 0) + (row * ny * nz + col) * per
    to = jnp.broadcast_to(r["order"][...].reshape(1, per), (per, per))
    r["hot"][...] = jnp.where(source == to, 1.0, 0.0).T.astype(BF)

    pl.semaphore_wait(barrier, len(peers))

    def remote(src, dst, s, t, to):
        return pltpu.make_async_remote_copy(
            src_ref=src, dst_ref=dst, send_sem=s, recv_sem=t, device_id=to, device_id_type=MESH
        )

    def reduce(comm, ref, scratch, turn):
        steps = len(comm.axes)
        count = len(comm.messages)
        slot = {m: i for i, m in enumerate(comm.messages)}
        recv = [scratch[p * count : (p + 1) * count] for p in range(len(comm.parts))]
        sends = r["send_sem"].at[turn]
        full = (1 << steps) - 1

        def copy(p, j, mask, d):
            order, r0, rows = comm.parts[p]
            a = order[j]
            index = comm.span(order, mask, {a: d})
            return remote(
                ref(index, pl.ds(r0, rows)),
                recv[p][slot[j, mask]].at[d - 1],
                sends,
                r["recv_sem"].at[turn, p, slot[j, mask]],
                device(a, d, comm.n[a]),
            )

        def send(p, j, mask):
            for d in range(1, comm.n[comm.parts[p][0][j]]):
                copy(p, j, mask, d).start()

        arrived = set()

        def wait(p, j, mask):
            if (p, j, mask) not in arrived:
                arrived.add((p, j, mask))
                buf = recv[p][slot[j, mask]]
                sem = r["recv_sem"].at[turn, p, slot[j, mask]]
                remote(buf, buf, sends, sem, partner).wait_recv()

        def total(p, mask, low):
            order, r0, rows = comm.parts[p]
            froms = [recv[p][slot[j, mask]] for j in range(low, steps)]
            for j in range(low, steps):
                wait(p, j, mask)
            axes = [a for a in comm.axes if mask >> order.index(a) & 1]
            dims = [comm.n[a] - 1 for a in axes]

            def one(at):
                index = {a: 0 for a in order}
                for a, where in zip(axes, at):
                    index[a] = where + 1
                here = ref(index, pl.ds(r0, rows))
                value = here[...].astype(F32)
                for buf in froms:
                    for d in range(buf.shape[0]):
                        value = value + buf[(d, *at)].astype(F32)
                return here, value

            if not axes:
                return one(())[1]
            if len(dims) == 1:
                for i in range(dims[0]):
                    here, value = one((i,))
                    here[...] = value.astype(BF)
            else:

                @pl.loop(0, dims[0])
                def _(i):
                    for k in range(dims[1]):
                        here, value = one((i, k))
                        here[...] = value.astype(BF)

        parts = range(len(comm.parts))
        last = steps - 1
        order_of = sorted(range(2**last), key=lambda m: -bin(m).count("1"))
        for mask in order_of:
            for p in parts:
                send(p, last, mask)
        for i in reversed(range(last)):
            for mask in sorted(range(2**i), key=lambda m: -bin(m).count("1")):
                for p in parts:
                    total(p, mask | 1 << i, i + 1)
                    send(p, i, mask)
        out = [total(p, 0, 0) for p in parts]
        sent = sum((comm.blocks - 1) * rows for _, _, rows in comm.parts)
        everything = drain(sent)
        remote(everything, everything, sends, r["recv_sem"].at[turn, 0, 0], partner).wait_send()
        return [(r0, rows, out[p]) for p, (_, r0, rows) in enumerate(comm.parts)]

    def drain(rows):
        return r["al"].at[pl.ds(0, rows // 128)]

    def gather(level, value, buf, turn):
        comm = comms[level]
        steps = len(comm.axes)
        slot = {m: i for i, m in enumerate(comm.messages)}
        sends = r["send_sem"].at[turn]
        d2d_send = r["d2d_send"].at[turn]
        d2d_recv = r["d2d_recv"].at[turn]

        def block(index, side, rows):
            return buf.at[(index.get("x", 0), side, index["y"], index["z"], rows)]

        buf[0, 0, 0, 0] = value

        def send(p, j, mask):
            order, r0, rows = comm.parts[p]
            a = order[j]
            n = comm.n[a]
            src = block(comm.span(order, mask, {}), 0, pl.ds(r0, rows))
            for d in range(1, n):
                dst = block(comm.span(order, mask, {a: n - d}), 0, pl.ds(r0, rows))
                remote(src, dst, sends, r["recv_sem"].at[turn, p, slot[j, mask]], device(a, d, n)).start()

        def arrive(p, j, mask):
            order, r0, rows = comm.parts[p]
            index = comm.span(order, mask | 1 << j, {})
            got = block(index, 0, pl.ds(r0, rows))
            remote(got, got, sends, r["recv_sem"].at[turn, p, slot[j, mask]], partner).wait_recv()
            for k in range(j + 1, steps):
                send(p, k, mask | 1 << j)
            remote(got, block(index, 1, pl.ds(r0, rows)), d2d_send, d2d_recv, partner).start()

        parts = range(len(comm.parts))
        for j in range(steps):
            for p in parts:
                send(p, j, 0)
        remote(buf.at[0, 0, 0, 0], buf.at[0, 1, 0, 0], d2d_send, d2d_recv, partner).start()
        for j, mask in sorted(comm.messages, key=lambda m: (bin(m[1]).count("1"), m[0])):
            for p in parts:
                arrive(p, j, mask)
        sent = sum((comm.blocks - 1) * rows for _, _, rows in comm.parts)
        everything = drain(sent)
        remote(everything, everything, sends, r["recv_sem"].at[turn, 0, 0], partner).wait_send()
        remote(buf.at[:, 0], buf.at[:, 1], d2d_send, d2d_recv, partner).wait()

    offsets = cfg["offsets"]
    natural = [
        ((yi + ny - coord["y"]) % ny, (zi + nz - coord["z"]) % nz) for yi in range(ny) for zi in range(nz)
    ]

    def place(nx, dx, side, dy, dz):
        xi = (coord["x"] % nx + dx) % nx
        ci = (core + side) % CORES
        return ((xi * CORES + ci) * ny + (coord["y"] + dy) % ny) * nz + (coord["z"] + dz) % nz

    def triangle(level, buf, lower):
        off = offsets[level]
        fronts = groups0 * 2**level
        me = row % fronts

        def panel(g):
            return r["tri_buf"][:, pl.ds(pl.multiple_of(off + g * plane, 128), plane)]

        nx = buf.shape[0]

        def vector(g):
            dx = (g // CORES + nx - coord["x"] % nx) % nx
            side = (g + core) % CORES
            return jnp.concatenate([buf[dx, side, dy, dz] for dy, dz in natural], 0)

        row_ids = col * seg + lax.broadcasted_iota(jnp.int32, (seg, plane), 0)
        col_ids = lax.broadcasted_iota(jnp.int32, (seg, plane), 1)
        keep = col_ids < row_ids if lower else col_ids >= row_ids
        masked = jnp.where(keep, panel(me).astype(F32), 0.0).astype(BF)
        acc = dot(masked, vector(me))

        def more(g, acc):
            return acc + dot(panel(g), vector(g))

        if lower:
            return lax.fori_loop(0, me, more, acc)
        return lax.fori_loop(me + 1, fronts, more, acc)

    get_idx = []
    for k in range(levels - 1):
        m = cfg["offsets"][k + 1] - cfg["offsets"][k]
        first = pl.multiple_of(k * (r["updates"].shape[0] // (levels - 1)) + row // 2 ** (k + 1) * m, 1024)
        at = pl.ds(cfg["offsets"][k], m)
        get_idx.append(pltpu.make_async_copy(r["updates"].at[pl.ds(first, m)], r["targets"].at[at], load.at[3 + k]))
    get_a.wait()
    for copy in (get_p, get_w, *get_idx):
        copy.start()
    al, sol, tb = r["al"], r["gathered"], r["tb"]
    kb = r["where"].shape[1]
    bpd = per // 128
    group = bpd * ny * nz

    def block_at(i, s):
        b = r["where"][i, s]
        return sol[b // group * bpd + b % bpd]

    @pl.loop(0, ny * nz)
    def _(c):
        dy, dz = c // nz, c % nz
        to = (coord["y"] + dy) % ny * nz + (coord["z"] + dz) % nz
        for j in range(bpd):
            i = to * bpd + j
            left = jnp.concatenate([al[i * kb + s] for s in range(kb)], 1)
            right = jnp.concatenate([block_at(i, s) for s in range(kb)], 0)
            tb[dy, dz, j * 128 : (j + 1) * 128, :] = dot(left, right).astype(BF)

    get_l = pltpu.make_async_copy(r["placed"], al, load.at[0])
    get_l.start()

    def first_b(index, rows):
        return tb.at[(index["y"], index["z"], rows)]

    for r0, rows, value in reduce(comm_b, first_b, r["sum_b"], 0):
        at = slice(r0, r0 + rows)
        r["product"][at, :] = value
        res = r["rhs"][at, :] - value
        hi = res.astype(BF)
        r["split"][at, 0:128] = hi
        r["split"][at, 128:256] = (res - hi.astype(F32)).astype(BF)
    both = dot(r["hot"][...], r["split"][...])
    r["vee"][...] = both[:, 0:128] + both[:, 128:256]

    get_p.wait()
    turn = 1
    buf_a, buf_b = r["buf_a"], r["buf_b"]
    incoming = None
    for level in range(levels):
        e = r["vee"][level * seg : (level + 1) * seg, :]
        if level > 0:
            parts = incoming
            for r0, rows, value in parts:
                r["minus"][r0 : r0 + rows, :] = value
            e = e - r["minus"][...]
        cb = e.astype(BF)
        gather(level, cb, buf_a[level], turn)
        turn += 1
        y = (triangle(level, buf_a[level], True) + cb.astype(F32)).astype(BF)
        r["why"][level] = y
        if level == 0:
            get_l.wait()
        if level + 1 < levels:
            t, rd = r["t"][level], r["rd"][level]
            nx = t.shape[0]
            base = 2 * offsets[level] // 128
            half = ny // 2

            def update(dx, side, t=t, base=base, y=y, nx=nx):
                for h in range(2):
                    spots = [(dy, dz) for dy in range(h * half, (h + 1) * half) for dz in range(nz)]
                    rows = [al[base + place(nx, dx, side, dy, dz)] for dy, dz in spots]
                    res = dot(jnp.concatenate(rows, 0), y).astype(BF)
                    t[dx, side, h * half : (h + 1) * half] = res.reshape(half, nz, 128, 128)

            d2d_send, d2d_recv = r["d2d_send"].at[turn], r["d2d_recv"].at[turn]
            for xi in range(nx):
                update(xi, 1)
                remote(t.at[xi, 1], rd.at[xi], d2d_send, d2d_recv, partner).start()
            for xi in range(nx):
                update(xi, 0)
            remote(t.at[:, 1], rd, d2d_send, d2d_recv, partner).wait()

            @pl.loop(0, nx * ny)
            def _(i, t=t, rd=rd):
                xi, yi = i // ny, i % ny
                for zi in range(nz):
                    value = t[xi, 0, yi, zi].astype(F32) + rd[xi, yi, zi].astype(F32)
                    t[xi, 0, yi, zi] = value.astype(BF)

            def first(index, rows, t=t):
                return t.at[(index["x"], 0, index["y"], index["z"], rows)]

            incoming = reduce(comms[level + 1], first, r["sums"][level], turn)
            turn += 1

    for copy in (get_w, *get_idx):
        copy.wait()
    xb = None
    for level in reversed(range(levels)):
        z = r["why"][level]
        if level + 1 < levels:
            src = buf_a[level + 1]
            wide, picked = r["wide"], r["picked"]
            xs = src.shape[0]

            @pl.loop(0, xs * CORES * ny)
            def _(i, src=src, xs=xs):
                dx, side, dy = i // (CORES * ny), i // ny % CORES, i % ny
                for dz in range(nz):
                    to = pl.multiple_of(place(xs, dx, side, dy, dz) * 128, 128)
                    wide[pl.ds(to, 128), :] = src[dx, side, dy, dz].astype(F32)

            m = offsets[level + 1] - offsets[level]
            tile = picked.shape[0]
            tiles = m // tile // CORES
            where = r["targets"]
            step = 32
            rows = r["rows"]
            d2d_send, d2d_recv = r["d2d_send"].at[turn], r["d2d_recv"].at[turn]

            def product(i, acc, level=level):
                at = pl.ds(pl.multiple_of(offsets[level] + i * tile, 128), tile)
                return acc + dot(r["upper_buf"][:, at], rows[i])

            def chunk(i, acc, level=level, tiles=tiles):
                mine = core * tiles + i
                first = offsets[level] + mine * tile

                @pl.loop(0, tile // step)
                def _(u):
                    for v in range(step):
                        w = u * step + v
                        picked[w] = wide[where[first + w]]

                rows[mine] = picked[...].astype(BF)
                remote(rows.at[mine], rows.at[mine], d2d_send, d2d_recv, partner).start()
                return product(mine, acc)

            total = lax.fori_loop(0, tiles, chunk, jnp.zeros((seg, 128), F32))
            sent, got = rows.at[pl.ds(core * tiles, tiles)], rows.at[pl.ds(other * tiles, tiles)]
            remote(sent, got, d2d_send, d2d_recv, partner).wait()
            total = lax.fori_loop(other * tiles, (other + 1) * tiles, product, total)
            turn += 1
            z = (z.astype(F32) - total).astype(BF)
        gather(level, z, buf_b[level], turn)
        turn += 1
        x = triangle(level, buf_b[level], False)
        at = slice(level * seg, (level + 1) * seg)
        r["correction"][at, :] = x
        if level > 0:
            gather(level, x.astype(BF), buf_a[level], turn)
            turn += 1


def refine(levels, nx, ny, nz, gathered, rhs, blocks, where, order, tri, placed, upper, updates):
    per = rhs.shape[0]
    seg = per // levels
    cols = ny * nz
    groups0 = CORES
    span0 = groups0 * cols * seg
    offsets = [span0 * (2**k - 1) for k in range(levels + 1)]
    comms = [Comm({"x": 2**k, "y": ny, "z": nz}, seg) for k in range(levels)]
    comm_b = Comm({"x": 1, "y": ny, "z": nz}, per)
    turns = 5 * levels - 2
    vmem = pl.BlockSpec(memory_space=pltpu.VMEM)
    smem = pl.BlockSpec(memory_space=pltpu.SMEM)
    hbm = pl.BlockSpec(memory_space=pl.ANY)
    ins = [
        ("gathered", vmem), ("rhs", vmem), ("blocks", hbm), ("where", smem), ("order", vmem),
        ("tri", hbm), ("placed", hbm), ("upper", hbm), ("updates", hbm),
    ]
    names = [n for n, _ in ins]
    in_specs = [s for _, s in ins]
    names += ["correction", "product"]
    front = lambda k: (2**k, CORES, ny, nz, seg, 128)
    scratch = {
        "al": pltpu.VMEM(blocks.shape, BF),
        "tri_buf": pltpu.VMEM(tri.shape, BF),
        "upper_buf": pltpu.VMEM(upper.shape, BF),
        "hot": pltpu.VMEM((per, per), BF),
        "tb": pltpu.VMEM((ny, nz, per, 128), BF),
        "split": pltpu.VMEM((per, 256), BF),
        "vee": pltpu.VMEM((per, 128), F32),
        "minus": pltpu.VMEM((seg, 128), F32),
        "why": pltpu.VMEM((levels, seg, 128), BF),
        "wide": pltpu.VMEM((2 ** (levels - 1) * span0, 128), F32),
        "picked": pltpu.VMEM((1024, 128), F32),
        "rows": pltpu.VMEM(((offsets[levels - 1] - offsets[levels - 2]) // 1024, 1024, 128), BF),
        "targets": pltpu.SMEM((offsets[levels - 1],), jnp.int32),
        "load_sem": pltpu.SemaphoreType.DMA((2 + levels,)),
        "send_sem": pltpu.SemaphoreType.DMA((turns,)),
        "recv_sem": pltpu.SemaphoreType.DMA((turns, 3, 7)),
        "d2d_send": pltpu.SemaphoreType.DMA((turns,)),
        "d2d_recv": pltpu.SemaphoreType.DMA((turns,)),
    }
    names += list(scratch)
    shapes = list(scratch.values())
    lists = {
        "buf_a": [pltpu.VMEM(front(k), BF) for k in range(levels)],
        "buf_b": [pltpu.VMEM(front(k), BF) for k in range(levels)],
        "t": [pltpu.VMEM(front(k + 1), BF) for k in range(levels - 1)],
        "rd": [pltpu.VMEM((2 ** (k + 1), ny, nz, seg, 128), BF) for k in range(levels - 1)],
        "sum_b": comm_b.sum_scratch(),
    }
    for k in range(levels - 1):
        lists[f"sums{k}"] = comms[k + 1].sum_scratch()
    for name, items in lists.items():
        names += [f"{name}.{i}" for i in range(len(items))]
        shapes += items

    def body(*refs):
        flat = dict(zip(names, refs))
        r = {n: v for n, v in flat.items() if "." not in n}
        for name, items in lists.items():
            r[name] = [flat[f"{name}.{i}"] for i in range(len(items))]
        r["sums"] = [r[f"sums{k}"] for k in range(levels - 1)]
        cfg = dict(
            names=list(r), levels=levels, groups0=groups0, nx=nx, ny=ny, nz=nz, seg=seg,
            comms=comms, comm_b=comm_b, offsets=offsets,
        )
        main_kernel(cfg, *r.values())

    return pl.pallas_call(
        body,
        out_shape=(jax.ShapeDtypeStruct(rhs.shape, F32), jax.ShapeDtypeStruct(rhs.shape, F32)),
        in_specs=in_specs,
        out_specs=(vmem, vmem),
        scratch_shapes=shapes,
        compiler_params=pltpu.CompilerParams(
            collective_id=0, has_side_effects=True, vmem_limit_bytes=67043328
        ),
        cost_estimate=pl.CostEstimate(flops=10**10, bytes_accessed=3 * 10**7, transcendentals=0),
        name="refine_step",
    )(gathered, rhs, blocks, where, order, tri, placed, upper, updates)


def on_device(
    solution,
    right_side,
    block_values,
    block_columns,
    row_order,
    tri_inverses,
    lower_updates,
    upper_updates,
    update_rows,
):
    row_count = lax.axis_size("row")
    col_count = lax.axis_size("col")
    levels = row_count.bit_length() - 1
    per = solution.shape[0]
    seg = per // levels
    block_size = block_values.shape[2]
    per_block = per // block_size
    gathered = sent_to_all(solution.astype(BF), "row").reshape(row_count * per_block, block_size, -1)
    span0 = CORES * col_count * seg
    updates = update_rows.reshape(-1)
    placed = place_rows(lower_updates, updates, [span0 * 2**k for k in range(levels - 1)])
    ny = math.isqrt(col_count)
    correction, product = refine(
        levels,
        row_count // CORES,
        ny,
        col_count // ny,
        gathered,
        right_side,
        block_values.reshape(-1, block_size, block_size),
        block_columns,
        row_order,
        tri_inverses,
        placed,
        upper_updates,
        updates,
    )
    return solution + correction, right_side - product


def solution(mesh):
    in_specs = (
        P(("row", "col"), None),
        P(("row", "col"), None),
        P("row", "col", None, None),
        P("row", "col"),
        P(("row", "col")),
        P(("row", "col"), None),
        P(None, ("row", "col")),
        P(("row", "col"), None),
        P(),
    )
    out_specs = (P(("row", "col"), None), P(("row", "col"), None))
    return jax.shard_map(
        on_device, mesh=mesh, in_specs=in_specs, out_specs=out_specs, check_vma=False
    )
```

time: 266 us -> 229 us (0.86)
  Pallas kernels: 249 us -> 213 us
  local copies, waits for them, and re-layouts: 8.04 us -> 3.92 us
    pallas_call x1, Pallas kernels: 228 us -> 197 us  [refine(): pl.pallas_call(body, out_shape=(jax.ShapeDtypeStruct(rhs.shape, F32), jax...]
    pallas_call x1, Pallas kernels: 20.9 us -> 16.8 us  [place_rows(): pl.pallas_call(functools.partial(place_kernel, spans), out_shape=jax.Shap...]
  transfers between devices with their start and end apart: 1 -> 1, of which waited for: 0 -> 0; matrix products, arithmetic and copies ran while one was open for 2% -> 1% of each run, Pallas kernels for 8% -> 7%
where the time goes in v2:
time: 229 us; the launch traced here: 228 us
  Pallas kernels  213 us (93%)
  starting transfers between devices  5.79 us (3%)
  other arithmetic  4.38 us (2%)
  local copies, waits for them, and re-layouts  3.92 us (2%)
    pallas_call x1, Pallas kernels, refine(): pl.pallas_call(body, out_shape=(jax.ShapeDtypeStruct(rhs.shape, F32), jax...  197 us
    pallas_call x1, Pallas kernels, place_rows(): pl.pallas_call(functools.partial(place_kernel, spans), out_shape=jax.Shap...  16.8 us
    all_to_all x1, starting transfers between devices, sent_to_all(): return lax.all_to_all(copies, axis, split_axis=0, concat_axis=0, tiled=True)  5.79 us
  transfers between devices with their start and end apart: 1, of which 0 were waited for; matrix products, arithmetic and copies ran while one was open for 1% of the time, Pallas kernels for 7%

profile of v2, /device:TPU:1, one launch (start us, length us, event | category | flops | bytes accessed | tf_op | source)
XLA Modules:
  0.0 228.2 jit_solution(11864413990645884252)
XLA Ops:
  0.6 0.9 convert_element_type.3
  1.6 1.0 broadcast_in_dim.3
  2.6 5.8 %all-to-all-start = ((bf16[8,384,128]{2,1,0:T(8,128)(2,1)}), bf16[8,384,128]{2,1,0:T(8,128)(2,1)}, u32[]{:S(2)}, u32[]{:S(2)}) async-start(bf16[8,384,128]{2,1,0:T(8,128)(2,1)} %broadcast_in_dim.3), calls=%async_computation | async-start | bytes 1572864 | tf_op jit(solution)/shard_map/all_to_all | solution.py:19
  8.3 1.4 copy.11.refs_3_
  9.7 1.6 copy.12
  11.3 16.8 %place_rows.1.refs_6_ = bf16[192,128,128]{2,1,0:T(8,128)(2,1)} custom-call(bf16[12288,128]{1,0:T(8,128)(2,1)} %lower.1, s32[32768]{0:T(1024)} %bitcast.5), custom_call_target="tpu_custom_call" | custom-call | flops 10000000000 | bytes 10000000 | tf_op jit(solution)/shard_map/place_rows/pallas_call | solution.py:86
  28.1 0.0 all-to-all-done
  28.1 196.7 %refine_step.1 = (f32[384,128]{1,0:T(8,128)}, f32[384,128]{1,0:T(8,128)}) custom-call(bf16[24,128,128]{2,1,0:T(8,128)(2,1)} %bitcast.refs_0_, f32[384,128]{1,0:T(8,128)} %refs_1_.1, bf16[192,128,128]{2,1,0:T(8,128)(2,1)} %bitcast.7, s32[48,4]{1,0:T(8,128)} %copy.11.refs_3_, s32[384]{0:T(512)} %refs_4_.1, bf16[128,28672]{1,0:T(8,128)(2,1)} %refs_5_.1, ...), custom_call_target="tpu_custom_call" | custom-call | flops 10000000000 | bytes 30000000 | tf_op jit(solution)/shard_map/refine_step/pallas_call | solution.py:584
  224.8 1.7 add.3
  226.5 1.7 sub.3
Async XLA Ops:
  2.6 25.5 %all-to-all-start = ((bf16[8,384,128]{2,1,0:T(8,128)(2,1)}), bf16[8,384,128]{2,1,0:T(8,128)(2,1)}, u32[]{:S(2)}, u32[]{:S(2)}) async-start(bf16[8,384,128]{2,1,0:T(8,128)(2,1)} %broadcast_in_dim.3), calls=%async_computation | async-start | bytes 1572864 | tf_op jit(solution)/shard_map/all_to_all | solution.py:19

commit v3 on v2

--- a/solution.py
+++ b/solution.py
@@ -115,7 +115,7 @@
         else:
             third = rows * 3 // 8
             self.parts = [
-                (("x", "y", "z"), 0, third),
+                (("y", "x", "z"), 0, third),
                 (("z", "x", "y"), third, third),
                 (("y", "z", "x"), 2 * third, rows - 2 * third),
             ]
@@ -173,24 +173,23 @@
         pl.semaphore_signal(barrier, inc=1, device_id=peer, device_id_type=MESH)
 
     load = r["load_sem"]
-    get_a = pltpu.make_async_copy(r["blocks"], r["al"], load.at[0])
-    get_a.start()
+    piece = r["blocks"].shape[0] // ny
+    get_a = []
+    for dy in [*range(1, ny), 0]:
+        at = pl.ds((coord["y"] + dy) % ny * piece, piece)
+        get_a.append(pltpu.make_async_copy(r["blocks"].at[at], r["al"].at[at], load.at[3 + levels + dy]))
+        get_a[-1].start()
     get_p = pltpu.make_async_copy(r["tri"], r["tri_buf"], load.at[1])
     get_w = pltpu.make_async_copy(r["upper"], r["upper_buf"], load.at[2])
 
     per = r["rhs"].shape[0]
-    source = lax.broadcasted_iota(jnp.int32, (per, per), 0) + (row * ny * nz + col) * per
-    to = jnp.broadcast_to(r["order"][...].reshape(1, per), (per, per))
-    r["hot"][...] = jnp.where(source == to, 1.0, 0.0).T.astype(BF)
-
-    pl.semaphore_wait(barrier, len(peers))
 
     def remote(src, dst, s, t, to):
         return pltpu.make_async_remote_copy(
             src_ref=src, dst_ref=dst, send_sem=s, recv_sem=t, device_id=to, device_id_type=MESH
         )
 
-    def reduce(comm, ref, scratch, turn):
+    def reduce(comm, ref, scratch, turn, ready):
         steps = len(comm.axes)
         count = len(comm.messages)
         slot = {m: i for i, m in enumerate(comm.messages)}
@@ -214,6 +213,10 @@
             for d in range(1, comm.n[comm.parts[p][0][j]]):
                 copy(p, j, mask, d).start()
 
+        def send_last(p, d):
+            for mask in sorted(range(2 ** (steps - 1)), key=lambda m: -bin(m).count("1")):
+                copy(p, steps - 1, mask, d).start()
+
         arrived = set()
 
         def wait(p, j, mask):
@@ -258,10 +261,7 @@
 
         parts = range(len(comm.parts))
         last = steps - 1
-        order_of = sorted(range(2**last), key=lambda m: -bin(m).count("1"))
-        for mask in order_of:
-            for p in parts:
-                send(p, last, mask)
+        ready(send_last)
         for i in reversed(range(last)):
             for mask in sorted(range(2**i), key=lambda m: -bin(m).count("1")):
                 for p in parts:
@@ -281,13 +281,17 @@
         steps = len(comm.axes)
         slot = {m: i for i, m in enumerate(comm.messages)}
         sends = r["send_sem"].at[turn]
-        d2d_send = r["d2d_send"].at[turn]
-        d2d_recv = r["d2d_recv"].at[turn]
+        d2d_send = r["d2d_send"].at[turn, 0]
+        d2d_recv = r["d2d_recv"].at[turn, 0]
 
         def block(index, side, rows):
             return buf.at[(index.get("x", 0), side, index["y"], index["z"], rows)]
 
         buf[0, 0, 0, 0] = value
+        parts = range(len(comm.parts))
+
+        def arrival(p, j, mask):
+            return r["recv_sem"].at[turn, p, slot[j, mask]]
 
         def send(p, j, mask):
             order, r0, rows = comm.parts[p]
@@ -296,67 +300,70 @@
             src = block(comm.span(order, mask, {}), 0, pl.ds(r0, rows))
             for d in range(1, n):
                 dst = block(comm.span(order, mask, {a: n - d}), 0, pl.ds(r0, rows))
-                remote(src, dst, sends, r["recv_sem"].at[turn, p, slot[j, mask]], device(a, d, n)).start()
-
-        def arrive(p, j, mask):
-            order, r0, rows = comm.parts[p]
-            index = comm.span(order, mask | 1 << j, {})
-            got = block(index, 0, pl.ds(r0, rows))
-            remote(got, got, sends, r["recv_sem"].at[turn, p, slot[j, mask]], partner).wait_recv()
-            for k in range(j + 1, steps):
-                send(p, k, mask | 1 << j)
-            remote(got, block(index, 1, pl.ds(r0, rows)), d2d_send, d2d_recv, partner).start()
-
-        parts = range(len(comm.parts))
+                remote(src, dst, sends, arrival(p, j, mask), device(a, d, n)).start()
+
         for j in range(steps):
             for p in parts:
                 send(p, j, 0)
         remote(buf.at[0, 0, 0, 0], buf.at[0, 1, 0, 0], d2d_send, d2d_recv, partner).start()
         for j, mask in sorted(comm.messages, key=lambda m: (bin(m[1]).count("1"), m[0])):
             for p in parts:
-                arrive(p, j, mask)
-        sent = sum((comm.blocks - 1) * rows for _, _, rows in comm.parts)
-        everything = drain(sent)
-        remote(everything, everything, sends, r["recv_sem"].at[turn, 0, 0], partner).wait_send()
-        remote(buf.at[:, 0], buf.at[:, 1], d2d_send, d2d_recv, partner).wait()
+                order, r0, rows = comm.parts[p]
+                index = comm.span(order, mask | 1 << j, {})
+                got = block(index, 0, pl.ds(r0, rows))
+                remote(got, got, sends, arrival(p, j, mask), partner).wait_recv()
+                if j + 1 < steps:
+                    send(p, j + 1, mask | 1 << j)
+                remote(got, block(index, 1, pl.ds(r0, rows)), d2d_send, d2d_recv, partner).start()
+            for k in range(j + 2, steps):
+                for p in parts:
+                    send(p, k, mask | 1 << j)
+
+        swap = remote(buf.at[:, 0], buf.at[:, 1], d2d_send, d2d_recv, partner)
+
+        def close():
+            swap.wait_send()
+            sent = drain(sum((comm.blocks - 1) * rows for _, _, rows in comm.parts))
+            remote(sent, sent, sends, arrival(0, 0, 0), partner).wait_send()
+
+        return swap.wait_recv, close
 
     offsets = cfg["offsets"]
     natural = [
         ((yi + ny - coord["y"]) % ny, (zi + nz - coord["z"]) % nz) for yi in range(ny) for zi in range(nz)
     ]
 
-    def place(nx, dx, side, dy, dz):
+    def place(nx, dx, ci, dy, dz):
         xi = (coord["x"] % nx + dx) % nx
-        ci = (core + side) % CORES
         return ((xi * CORES + ci) * ny + (coord["y"] + dy) % ny) * nz + (coord["z"] + dz) % nz
 
-    def triangle(level, buf, lower):
+    def triangle(level, buf, lower, joined):
         off = offsets[level]
-        fronts = groups0 * 2**level
-        me = row % fronts
-
-        def panel(g):
-            return r["tri_buf"][:, pl.ds(pl.multiple_of(off + g * plane, 128), plane)]
-
         nx = buf.shape[0]
-
-        def vector(g):
-            dx = (g // CORES + nx - coord["x"] % nx) % nx
-            side = (g + core) % CORES
+        here = coord["x"] % nx
+
+        def panel(xi, ci):
+            return r["tri_buf"][:, pl.ds(pl.multiple_of(off + (xi * CORES + ci) * plane, 128), plane)]
+
+        def vector(xi, side):
+            dx = (xi + nx - here) % nx
             return jnp.concatenate([buf[dx, side, dy, dz] for dy, dz in natural], 0)
 
-        row_ids = col * seg + lax.broadcasted_iota(jnp.int32, (seg, plane), 0)
-        col_ids = lax.broadcasted_iota(jnp.int32, (seg, plane), 1)
-        keep = col_ids < row_ids if lower else col_ids >= row_ids
-        masked = jnp.where(keep, panel(me).astype(F32), 0.0).astype(BF)
-        acc = dot(masked, vector(me))
-
-        def more(g, acc):
-            return acc + dot(panel(g), vector(g))
+        acc = dot(r["masked"][level, int(lower)], vector(here, 0))
+
+        def mine(xi, acc):
+            return acc + dot(panel(xi, core), vector(xi, 0))
+
+        def theirs(xi, acc):
+            return acc + dot(panel(xi, other), vector(xi, 1))
 
         if lower:
-            return lax.fori_loop(0, me, more, acc)
-        return lax.fori_loop(me + 1, fronts, more, acc)
+            acc = lax.fori_loop(0, here, mine, acc)
+            joined()
+            return lax.fori_loop(0, here + core, theirs, acc)
+        acc = lax.fori_loop(here + 1, nx, mine, acc)
+        joined()
+        return lax.fori_loop(here + core, nx, theirs, acc)
 
     get_idx = []
     for k in range(levels - 1):
@@ -364,9 +371,6 @@
         first = pl.multiple_of(k * (r["updates"].shape[0] // (levels - 1)) + row // 2 ** (k + 1) * m, 1024)
         at = pl.ds(cfg["offsets"][k], m)
         get_idx.append(pltpu.make_async_copy(r["updates"].at[pl.ds(first, m)], r["targets"].at[at], load.at[3 + k]))
-    get_a.wait()
-    for copy in (get_p, get_w, *get_idx):
-        copy.start()
     al, sol, tb = r["al"], r["gathered"], r["tb"]
     kb = r["where"].shape[1]
     bpd = per // 128
@@ -376,23 +380,49 @@
         b = r["where"][i, s]
         return sol[b // group * bpd + b % bpd]
 
-    @pl.loop(0, ny * nz)
-    def _(c):
-        dy, dz = c // nz, c % nz
-        to = (coord["y"] + dy) % ny * nz + (coord["z"] + dz) % nz
-        for j in range(bpd):
-            i = to * bpd + j
-            left = jnp.concatenate([al[i * kb + s] for s in range(kb)], 1)
-            right = jnp.concatenate([block_at(i, s) for s in range(kb)], 0)
-            tb[dy, dz, j * 128 : (j + 1) * 128, :] = dot(left, right).astype(BF)
+    def block_rows(dy):
+        for dz in range(nz):
+            to = (coord["y"] + dy) % ny * nz + (coord["z"] + dz) % nz
+            for j in range(bpd):
+                i = to * bpd + j
+                left = jnp.concatenate([al[i * kb + s] for s in range(kb)], 1)
+                right = jnp.concatenate([block_at(i, s) for s in range(kb)], 0)
+                tb[dy, dz, j * 128 : (j + 1) * 128, :] = dot(left, right).astype(BF)
+
+    def products(send):
+        for n, dy in enumerate([*range(1, ny), 0]):
+            get_a[n].wait()
+            block_rows(dy)
+            if n == 0:
+                pl.semaphore_wait(barrier, len(peers))
+            for p, (order, _, _) in enumerate(comm_b.parts):
+                if order[-1] == "y" and dy > 0:
+                    send(p, dy)
+        for p, (order, _, _) in enumerate(comm_b.parts):
+            if order[-1] == "z":
+                for dz in range(1, nz):
+                    send(p, dz)
+        for copy in (get_l, get_p, get_w, *get_idx):
+            copy.start()
+
+        source = lax.broadcasted_iota(jnp.int32, (per, per), 0) + (row * ny * nz + col) * per
+        to = jnp.broadcast_to(r["order"][...].reshape(1, per), (per, per))
+        r["hot"][...] = jnp.where(source == to, 1.0, 0.0).T.astype(BF)
+        get_p.wait()
+        for level in range(levels):
+            here = coord["x"] % 2**level * CORES + core
+            own = r["tri_buf"][:, pl.ds(pl.multiple_of(offsets[level] + here * plane, 128), plane)].astype(F32)
+            row_ids = col * seg + lax.broadcasted_iota(jnp.int32, (seg, plane), 0)
+            col_ids = lax.broadcasted_iota(jnp.int32, (seg, plane), 1)
+            r["masked"][level, 0] = jnp.where(col_ids >= row_ids, own, 0.0).astype(BF)
+            r["masked"][level, 1] = jnp.where(col_ids < row_ids, own, 0.0).astype(BF)
 
     get_l = pltpu.make_async_copy(r["placed"], al, load.at[0])
-    get_l.start()
 
     def first_b(index, rows):
         return tb.at[(index["y"], index["z"], rows)]
 
-    for r0, rows, value in reduce(comm_b, first_b, r["sum_b"], 0):
+    for r0, rows, value in reduce(comm_b, first_b, r["sum_b"], 0, products):
         at = slice(r0, r0 + rows)
         r["product"][at, :] = value
         res = r["rhs"][at, :] - value
@@ -402,7 +432,6 @@
     both = dot(r["hot"][...], r["split"][...])
     r["vee"][...] = both[:, 0:128] + both[:, 128:256]
 
-    get_p.wait()
     turn = 1
     buf_a, buf_b = r["buf_a"], r["buf_b"]
     incoming = None
@@ -414,9 +443,10 @@
                 r["minus"][r0 : r0 + rows, :] = value
             e = e - r["minus"][...]
         cb = e.astype(BF)
-        gather(level, cb, buf_a[level], turn)
+        joined, close = gather(level, cb, buf_a[level], turn)
         turn += 1
-        y = (triangle(level, buf_a[level], True) + cb.astype(F32)).astype(BF)
+        y = (triangle(level, buf_a[level], True, joined) + cb.astype(F32)).astype(BF)
+        close()
         r["why"][level] = y
         if level == 0:
             get_l.wait()
@@ -429,29 +459,46 @@
             def update(dx, side, t=t, base=base, y=y, nx=nx):
                 for h in range(2):
                     spots = [(dy, dz) for dy in range(h * half, (h + 1) * half) for dz in range(nz)]
-                    rows = [al[base + place(nx, dx, side, dy, dz)] for dy, dz in spots]
+                    rows = [al[base + place(nx, dx, (core + side) % CORES, dy, dz)] for dy, dz in spots]
                     res = dot(jnp.concatenate(rows, 0), y).astype(BF)
                     t[dx, side, h * half : (h + 1) * half] = res.reshape(half, nz, 128, 128)
 
-            d2d_send, d2d_recv = r["d2d_send"].at[turn], r["d2d_recv"].at[turn]
-            for xi in range(nx):
-                update(xi, 1)
-                remote(t.at[xi, 1], rd.at[xi], d2d_send, d2d_recv, partner).start()
-            for xi in range(nx):
-                update(xi, 0)
-            remote(t.at[:, 1], rd, d2d_send, d2d_recv, partner).wait()
-
-            @pl.loop(0, nx * ny)
-            def _(i, t=t, rd=rd):
-                xi, yi = i // ny, i % ny
-                for zi in range(nz):
-                    value = t[xi, 0, yi, zi].astype(F32) + rd[xi, yi, zi].astype(F32)
-                    t[xi, 0, yi, zi] = value.astype(BF)
+            comm = comms[level + 1]
+
+            def sums(send, t=t, rd=rd, nx=nx, comm=comm, turn=turn, update=update):
+                swaps = []
+                for xi in range(nx):
+                    update(xi, 1)
+                for p, (_, r0, rows) in enumerate(comm.parts):
+                    at = pl.ds(r0, rows)
+                    swap = remote(
+                        t.at[:, 1, :, :, at],
+                        rd.at[:, :, :, at],
+                        r["d2d_send"].at[turn, p],
+                        r["d2d_recv"].at[turn, p],
+                        partner,
+                    )
+                    swap.start()
+                    swaps.append(swap)
+                for xi in range(nx):
+                    update(xi, 0)
+                for p, (order, r0, rows) in enumerate(comm.parts):
+                    swaps[p].wait()
+
+                    @pl.loop(0, nx * ny)
+                    def _(i, at=slice(r0, r0 + rows)):
+                        xi, yi = i // ny, i % ny
+                        for zi in range(nz):
+                            value = t[xi, 0, yi, zi, at].astype(F32) + rd[xi, yi, zi, at].astype(F32)
+                            t[xi, 0, yi, zi, at] = value.astype(BF)
+
+                    for d in range(1, comm.n[order[-1]]):
+                        send(p, d)
 
             def first(index, rows, t=t):
                 return t.at[(index["x"], 0, index["y"], index["z"], rows)]
 
-            incoming = reduce(comms[level + 1], first, r["sums"][level], turn)
+            incoming = reduce(comm, first, r["sums"][level], turn, sums)
             turn += 1
 
     for copy in (get_w, *get_idx):
@@ -464,20 +511,25 @@
             wide, picked = r["wide"], r["picked"]
             xs = src.shape[0]
 
-            @pl.loop(0, xs * CORES * ny)
-            def _(i, src=src, xs=xs):
-                dx, side, dy = i // (CORES * ny), i // ny % CORES, i % ny
-                for dz in range(nz):
-                    to = pl.multiple_of(place(xs, dx, side, dy, dz) * 128, 128)
-                    wide[pl.ds(to, 128), :] = src[dx, side, dy, dz].astype(F32)
-
+            for side in range(CORES):
+                if side == 1:
+                    joined()
+
+                @pl.loop(0, xs * ny)
+                def _(i, src=src, xs=xs, side=side):
+                    dx, dy = i // ny, i % ny
+                    for dz in range(nz):
+                        to = pl.multiple_of(place(xs, dx, (core + side) % CORES, dy, dz) * 128, 128)
+                        wide[pl.ds(to, 128), :] = src[dx, side, dy, dz].astype(F32)
+
+            close_x()
             m = offsets[level + 1] - offsets[level]
             tile = picked.shape[0]
             tiles = m // tile // CORES
             where = r["targets"]
             step = 32
             rows = r["rows"]
-            d2d_send, d2d_recv = r["d2d_send"].at[turn], r["d2d_recv"].at[turn]
+            d2d_send, d2d_recv = r["d2d_send"].at[turn, 0], r["d2d_recv"].at[turn, 0]
 
             def product(i, acc, level=level):
                 at = pl.ds(pl.multiple_of(offsets[level] + i * tile, 128), tile)
@@ -503,13 +555,14 @@
             total = lax.fori_loop(other * tiles, (other + 1) * tiles, product, total)
             turn += 1
             z = (z.astype(F32) - total).astype(BF)
-        gather(level, z, buf_b[level], turn)
+        joined, close = gather(level, z, buf_b[level], turn)
         turn += 1
-        x = triangle(level, buf_b[level], False)
+        x = triangle(level, buf_b[level], False, joined)
+        close()
         at = slice(level * seg, (level + 1) * seg)
         r["correction"][at, :] = x
         if level > 0:
-            gather(level, x.astype(BF), buf_a[level], turn)
+            joined, close_x = gather(level, x.astype(BF), buf_a[level], turn)
             turn += 1
 
 
@@ -541,6 +594,7 @@
         "hot": pltpu.VMEM((per, per), BF),
         "tb": pltpu.VMEM((ny, nz, per, 128), BF),
         "split": pltpu.VMEM((per, 256), BF),
+        "masked": pltpu.VMEM((levels, 2, seg, cols * seg), BF),
         "vee": pltpu.VMEM((per, 128), F32),
         "minus": pltpu.VMEM((seg, 128), F32),
         "why": pltpu.VMEM((levels, seg, 128), BF),
@@ -548,11 +602,11 @@
         "picked": pltpu.VMEM((1024, 128), F32),
         "rows": pltpu.VMEM(((offsets[levels - 1] - offsets[levels - 2]) // 1024, 1024, 128), BF),
         "targets": pltpu.SMEM((offsets[levels - 1],), jnp.int32),
-        "load_sem": pltpu.SemaphoreType.DMA((2 + levels,)),
+        "load_sem": pltpu.SemaphoreType.DMA((3 + levels + ny,)),
         "send_sem": pltpu.SemaphoreType.DMA((turns,)),
         "recv_sem": pltpu.SemaphoreType.DMA((turns, 3, 7)),
-        "d2d_send": pltpu.SemaphoreType.DMA((turns,)),
-        "d2d_recv": pltpu.SemaphoreType.DMA((turns,)),
+        "d2d_send": pltpu.SemaphoreType.DMA((turns, 3)),
+        "d2d_recv": pltpu.SemaphoreType.DMA((turns, 3)),
     }
     names += list(scratch)
     shapes = list(scratch.values())
@@ -593,6 +647,19 @@
         cost_estimate=pl.CostEstimate(flops=10**10, bytes_accessed=3 * 10**7, transcendentals=0),
         name="refine_step",
     )(gathered, rhs, blocks, where, order, tri, placed, upper, updates)
+
+
+def finish_kernel(old, rhs, correction, product, refined, residual):
+    refined[...] = old[...] + correction[...]
+    residual[...] = rhs[...] - product[...]
+
+
+def finish(*arrays):
+    vmem = pl.BlockSpec(memory_space=pltpu.VMEM)
+    out = jax.ShapeDtypeStruct(arrays[0].shape, F32)
+    return pl.pallas_call(
+        finish_kernel, out_shape=(out, out), in_specs=[vmem] * 4, out_specs=(vmem, vmem), name="finish"
+    )(*arrays)
 
 
 def on_device(
@@ -633,7 +700,7 @@
         upper_updates,
         updates,
     )
-    return solution + correction, right_side - product
+    return finish(solution, right_side, correction, product)
 
 
 def solution(mesh):

time: 229 us -> 226 us (0.987)
  other arithmetic: 4.38 us -> 0.94 us
where the time goes in v3:
time: 226 us; the launch traced here: 225 us
  Pallas kernels  214 us (95%)
  starting transfers between devices  5.79 us (3%)
  local copies, waits for them, and re-layouts  3.92 us (2%)
    pallas_call x1, Pallas kernels, refine(): pl.pallas_call(body, out_shape=(jax.ShapeDtypeStruct(rhs.shape, F32), jax...  195 us
    pallas_call x1, Pallas kernels, place_rows(): pl.pallas_call(functools.partial(place_kernel, spans), out_shape=jax.Shap...  16.8 us
    all_to_all x1, starting transfers between devices, sent_to_all(): return lax.all_to_all(copies, axis, split_axis=0, concat_axis=0, tiled=True)  5.79 us
  transfers between devices with their start and end apart: 1, of which 0 were waited for; matrix products, arithmetic and copies ran while one was open for 1% of the time, Pallas kernels for 7%

profile of v3, /device:TPU:1, one launch (start us, length us, event | category | flops | bytes accessed | tf_op | source)
XLA Modules:
  0.0 225.5 jit_solution(8295851176203663457)
XLA Ops:
  0.6 0.9 convert_element_type.3
  1.6 1.0 broadcast_in_dim.3
  2.6 5.8 %all-to-all-start = ((bf16[8,384,128]{2,1,0:T(8,128)(2,1)}), bf16[8,384,128]{2,1,0:T(8,128)(2,1)}, u32[]{:S(2)}, u32[]{:S(2)}) async-start(bf16[8,384,128]{2,1,0:T(8,128)(2,1)} %broadcast_in_dim.3), calls=%async_computation | async-start | bytes 1572864 | tf_op jit(solution)/shard_map/all_to_all | solution.py:19
  8.3 1.4 copy.11.refs_3_
  9.7 1.6 copy.12
  11.3 16.8 %place_rows.1.refs_6_ = bf16[192,128,128]{2,1,0:T(8,128)(2,1)} custom-call(bf16[12288,128]{1,0:T(8,128)(2,1)} %lower.1, s32[32768]{0:T(1024)} %bitcast.5), custom_call_target="tpu_custom_call" | custom-call | flops 10000000000 | bytes 10000000 | tf_op jit(solution)/shard_map/place_rows/pallas_call | solution.py:86
  28.1 0.0 all-to-all-done
  28.1 195.4 %refine_step.1 = (f32[384,128]{1,0:T(8,128)}, f32[384,128]{1,0:T(8,128)}) custom-call(bf16[24,128,128]{2,1,0:T(8,128)(2,1)} %bitcast.refs_0_, f32[384,128]{1,0:T(8,128)} %rhs.1, bf16[192,128,128]{2,1,0:T(8,128)(2,1)} %bitcast.7, s32[48,4]{1,0:T(8,128)} %copy.11.refs_3_, s32[384]{0:T(512)} %refs_4_.1, bf16[128,28672]{1,0:T(8,128)(2,1)} %refs_5_.1, ...), custom_call_target="tpu_custom_call" | custom-call | flops 10000000000 | bytes 30000000 | tf_op jit(solution)/shard_map/refine_step/pallas_call | solution.py:638
  223.5 2.0 finish.1
Async XLA Ops:
  2.6 25.5 %all-to-all-start = ((bf16[8,384,128]{2,1,0:T(8,128)(2,1)}), bf16[8,384,128]{2,1,0:T(8,128)(2,1)}, u32[]{:S(2)}, u32[]{:S(2)}) async-start(bf16[8,384,128]{2,1,0:T(8,128)(2,1)} %broadcast_in_dim.3), calls=%async_computation | async-start | bytes 1572864 | tf_op jit(solution)/shard_map/all_to_all | solution.py:19

commit v4 on v3

--- a/solution.py
+++ b/solution.py
@@ -25,7 +25,8 @@
 
 def place_kernel(spans, lower, updates, out, narrow, wide, placed, done, where, sem_in, sem_out, sem_idx):
     rows = 256
-    step = 32
+    step = 64
+    pieces = sem_out.shape[1]
     row = lax.axis_index("row")
     copies = []
     start = 0
@@ -63,14 +64,15 @@
                 placed[2 * start + where[u]] = wide[u]
 
         block = out.shape[1]
-        for part in range(2):
-            first = (2 * start + part * span) // block
-
-            @pl.loop(first, first + span // block)
+        size = 2 * span // pieces // block
+        for part in range(pieces):
+            first = 2 * start // block + part * size
+
+            @pl.loop(first, first + size)
             def _(i):
                 done[i] = placed[pl.ds(pl.multiple_of(i * block, block), block), :].astype(BF)
 
-            at = pl.ds(first, span // block)
+            at = pl.ds(first, size)
             put = pltpu.make_async_copy(done.at[at], out.at[at], sem_out.at[level, part])
             put.start()
             puts.append(put)
@@ -95,7 +97,7 @@
             pltpu.VMEM((blocks, 128, width), BF),
             pltpu.SMEM((total,), jnp.int32),
             pltpu.SemaphoreType.DMA((len(spans),)),
-            pltpu.SemaphoreType.DMA((len(spans), 2)),
+            pltpu.SemaphoreType.DMA((len(spans), 4)),
             pltpu.SemaphoreType.DMA((len(spans),)),
         ],
         compiler_params=pltpu.CompilerParams(vmem_limit_bytes=56 * 2**20),
@@ -527,7 +529,7 @@
             tile = picked.shape[0]
             tiles = m // tile // CORES
             where = r["targets"]
-            step = 32
+            step = 64
             rows = r["rows"]
             d2d_send, d2d_recv = r["d2d_send"].at[turn, 0], r["d2d_recv"].at[turn, 0]
 

time: 226 us -> 225 us (level)
  no operation moved by 1% of the time
where the time goes in v4:
time: 225 us
  Pallas kernels  213 us (95%)
  starting transfers between devices  5.79 us (3%)
  local copies, waits for them, and re-layouts  3.92 us (2%)
    pallas_call x1, Pallas kernels, refine(): pl.pallas_call(body, out_shape=(jax.ShapeDtypeStruct(rhs.shape, F32), jax...  195 us
    pallas_call x1, Pallas kernels, place_rows(): pl.pallas_call(functools.partial(place_kernel, spans), out_shape=jax.Shap...  15.8 us
    all_to_all x1, starting transfers between devices, sent_to_all(): return lax.all_to_all(copies, axis, split_axis=0, concat_axis=0, tiled=True)  5.79 us
  transfers between devices with their start and end apart: 1, of which 0 were waited for; matrix products, arithmetic and copies ran while one was open for 1% of the time, Pallas kernels for 7%

profile of v4, /device:TPU:1, one launch (start us, length us, event | category | flops | bytes accessed | tf_op | source)
XLA Modules:
  0.0 224.5 jit_solution(6530708033301866927)
XLA Ops:
  0.6 0.9 convert_element_type.3
  1.6 1.0 broadcast_in_dim.3
  2.6 5.8 %all-to-all-start = ((bf16[8,384,128]{2,1,0:T(8,128)(2,1)}), bf16[8,384,128]{2,1,0:T(8,128)(2,1)}, u32[]{:S(2)}, u32[]{:S(2)}) async-start(bf16[8,384,128]{2,1,0:T(8,128)(2,1)} %broadcast_in_dim.3), calls=%async_computation | async-start | bytes 1572864 | tf_op jit(solution)/shard_map/all_to_all | solution.py:19
  8.3 1.4 copy.11.refs_3_
  9.7 1.6 copy.12
  11.3 15.8 %place_rows.1.refs_6_ = bf16[192,128,128]{2,1,0:T(8,128)(2,1)} custom-call(bf16[12288,128]{1,0:T(8,128)(2,1)} %lower.1, s32[32768]{0:T(1024)} %bitcast.5), custom_call_target="tpu_custom_call" | custom-call | flops 10000000000 | bytes 10000000 | tf_op jit(solution)/shard_map/place_rows/pallas_call | solution.py:88
  27.1 0.0 all-to-all-done
  27.1 195.5 %refine_step.1 = (f32[384,128]{1,0:T(8,128)}, f32[384,128]{1,0:T(8,128)}) custom-call(bf16[24,128,128]{2,1,0:T(8,128)(2,1)} %bitcast.refs_0_, f32[384,128]{1,0:T(8,128)} %rhs.1, bf16[192,128,128]{2,1,0:T(8,128)(2,1)} %bitcast.7, s32[48,4]{1,0:T(8,128)} %copy.11.refs_3_, s32[384]{0:T(512)} %refs_4_.1, bf16[128,28672]{1,0:T(8,128)(2,1)} %refs_5_.1, ...), custom_call_target="tpu_custom_call" | custom-call | flops 10000000000 | bytes 30000000 | tf_op jit(solution)/shard_map/refine_step/pallas_call | solution.py:640
  222.5 2.0 finish.1
Async XLA Ops:
  2.6 24.5 %all-to-all-start = ((bf16[8,384,128]{2,1,0:T(8,128)(2,1)}), bf16[8,384,128]{2,1,0:T(8,128)(2,1)}, u32[]{:S(2)}, u32[]{:S(2)}) async-start(bf16[8,384,128]{2,1,0:T(8,128)(2,1)} %broadcast_in_dim.3), calls=%async_computation | async-start | bytes 1572864 | tf_op jit(solution)/shard_map/all_to_all | solution.py:19
